TPU v7x, 8 devices: a whole 2x2x1 slice. The times are simulated.
8 devices in a mesh: terms: 8 (over z, y, x, core).
Axes of the slice: x: 2, y: 2, z: 1, core: 2. Of those that a mesh axis runs over, the one named last changes fastest.
Arguments:
- wavefunction: float32 [768, 16, 768], replicated
- left_env: bfloat16 [32, 768, 768], P('terms')
- pair_ops: bfloat16 [32, 16, 16], P('terms')
- right_env: bfloat16 [32, 768, 768], P('terms')
- full_term: int32 [32], P('terms')
Outputs:
- output 1: float32 [7, 768, 16, 768], P(None, 'terms')
- output 2: float32 [6], replicated
- output 3: float32 [6], replicated
All inputs are finite; a program needn't handle non-finite values.
Results may differ from a plain program's by a relative error of at most 0.0114484.
Values are sent between devices in bfloat16 or wider.
A program may use at most 1 GiB of HBM per device.

v0:
```python
import functools

import jax
import jax.numpy as jnp
from jax import lax
from jax.experimental import pallas as pl
from jax.experimental.pallas import tpu as pltpu
from jax.sharding import PartitionSpec as P


LANCZOS_STEPS = 6
AXIS_NAME = 'terms'
GROUP = 4
CHUNK = 256
ROW_TILE = 16
BF16 = jnp.bfloat16
F32 = jnp.float32
FIN_BLOCKS = 4


def one_sided_body(order_ref, split_ref, *rest, parts, resume):
    u_refs = rest[:parts]
    pair_ref = rest[parts]
    left_refs = rest[parts + 1:parts + 1 + GROUP * parts]
    rest = rest[parts + 1 + GROUP * parts:]
    if resume:
        sigma_in, rest = rest[0], rest[1:]
    rest = rest[1:]
    sigma_out, _, sigma_ref, z_ref, in_sem, out_sem = rest
    grp = pl.program_id(0)
    nq, nb, nc = u_refs[0].shape
    na = sigma_ref.shape[2]
    half = nq // 2
    last = jnp.maximum(split_ref[0] - 1, 0)

    @pl.when(grp == 0)
    def _():
        if resume:
            copy = pltpu.make_async_copy(sigma_in, sigma_ref, in_sem)
            copy.start()
            copy.wait()
        else:
            sigma_ref[...] = jnp.zeros_like(sigma_ref)

    @pl.when(grp < split_ref[0])
    def _():
        pair = pair_ref[...].reshape(GROUP * nq * ROW_TILE, nq * ROW_TILE)
        for ci in range(parts):
            for bt in range(nb // ROW_TILE):
                rows = pl.ds(bt * ROW_TILE, ROW_TILE)
                y = u_refs[ci][:, rows, :].reshape(nq * ROW_TILE, nc)
                z = jnp.dot(pair, y, preferred_element_type=F32).astype(BF16)
                z = z.reshape(GROUP, nq, ROW_TILE, nc)
                for t in range(GROUP):
                    z_ref[:, rows, (ci * GROUP + t) * nc:(ci * GROUP + t + 1) * nc] = z[t]

    for h in range(2):
        @pl.when(grp < split_ref[0])
        def _():
            left = jnp.concatenate([left_refs[ci * GROUP + t][0] for ci in range(parts) for t in range(GROUP)], axis=0)
            zs = z_ref[h * half:(h + 1) * half].reshape(half * nb, parts * GROUP * nc)
            prod = jnp.dot(zs, left, preferred_element_type=F32).reshape(half, nb, na)
            sigma_ref[h * half:(h + 1) * half] += prod

        @pl.when(grp == last)
        def _():
            pltpu.make_async_copy(sigma_ref.at[pl.ds(h * half, half)], sigma_out.at[pl.ds(h * half, half)], out_sem.at[h]).start()

    @pl.when(grp == last)
    def _():
        for h in range(2):
            pltpu.make_async_copy(sigma_ref.at[pl.ds(h * half, half)], sigma_out.at[pl.ds(h * half, half)], out_sem.at[h]).wait()


def full_body(order_ref, split_ref, u_hbm, right_ref, pair_ref, *rest, gathered):
    left_refs = rest[:GROUP]
    sigma_in, _, sigma_out, _, sigma_ref, u_ref, y_ref, z_ref, u_sem, in_sem, out_sem = rest[GROUP:]
    grp = pl.program_id(0)
    num_grp = pl.num_programs(0)
    nq, nb, na = sigma_ref.shape
    nd = right_ref.shape[2]
    nc = u_ref.shape[-1]
    half = nq // 2

    def u_copy(r):
        if gathered:
            return pltpu.make_async_copy(u_hbm.at[:, r], u_ref.at[:, r], u_sem.at[r])
        return pltpu.make_async_copy(u_hbm.at[r], u_ref.at[r], u_sem.at[r])

    @pl.when((grp == 0) & (split_ref[0] < num_grp))
    def _():
        for r in range(nq):
            u_copy(r).start()
        pltpu.make_async_copy(sigma_in, sigma_ref, in_sem).start()

    @pl.when(grp == split_ref[0])
    def _():
        for r in range(nq):
            u_copy(r).wait()

    @pl.when(grp >= split_ref[0])
    def _():
        right = right_ref[...].reshape(GROUP * nb, nd)
        for r in range(nq):
            u = (u_ref[:, r] if gathered else u_ref[r]).reshape(nd, nc)
            y_ref[r] = jnp.dot(right, u, preferred_element_type=F32).astype(BF16)
        for t in range(GROUP):
            for bt in range(nb // ROW_TILE):
                y = y_ref[:, pl.ds(t * nb + bt * ROW_TILE, ROW_TILE), :].reshape(nq * ROW_TILE, nc)
                z = jnp.dot(pair_ref[t], y, preferred_element_type=F32).astype(BF16)
                z_ref[:, pl.ds(bt * ROW_TILE, ROW_TILE), t * nc:(t + 1) * nc] = z.reshape(nq, ROW_TILE, nc)

    @pl.when(grp == split_ref[0])
    def _():
        pltpu.make_async_copy(sigma_in, sigma_ref, in_sem).wait()

    for h in range(2):
        @pl.when(grp >= split_ref[0])
        def _():
            left = jnp.concatenate([left_refs[t][0] for t in range(GROUP)], axis=0)
            zs = z_ref[h * half:(h + 1) * half].reshape(half * nb, GROUP * nc)
            prod = jnp.dot(zs, left, preferred_element_type=F32).reshape(half, nb, na)
            sigma_ref[h * half:(h + 1) * half] += prod

        @pl.when((grp == num_grp - 1) & (split_ref[0] < num_grp))
        def _():
            pltpu.make_async_copy(sigma_ref.at[pl.ds(h * half, half)], sigma_out.at[pl.ds(h * half, half)], out_sem.at[h]).start()

    @pl.when((grp == num_grp - 1) & (split_ref[0] < num_grp))
    def _():
        for h in range(2):
            pltpu.make_async_copy(sigma_ref.at[pl.ds(h * half, half)], sigma_out.at[pl.ds(h * half, half)], out_sem.at[h]).wait()


ANY = pl.BlockSpec(memory_space=pl.ANY)
VMEM_LIMIT = 63 << 20


def whole(shape):
    return pl.BlockSpec(shape, lambda g, o, s: (0,) * len(shape), pipeline_mode=pl.Buffered(1))


def one_sided_call(order, split, u_parts, pair_blk, left_parts, carried, sigma=None):
    parts = len(u_parts)
    nq, nb, nc = u_parts[0].shape
    na = left_parts[0].shape[2]
    terms = pair_blk.shape[0]
    nk = nq * ROW_TILE

    def clamp(g, s):
        return jnp.minimum(g, jnp.maximum(s[0] - 1, 0))

    left_specs = [pl.BlockSpec((1, nc, na), functools.partial(lambda g, o, s, t: (o[clamp(g, s) * GROUP + t], 0, 0), t=t))
                  for _ in range(parts) for t in range(GROUP)]
    resume = sigma is not None
    n = terms // 2
    first = 2 + parts + 1 + GROUP * parts
    aliases = {first: 0, first + 1: 1} if resume else {first: 1}
    return pl.pallas_call(
        functools.partial(one_sided_body, parts=parts, resume=resume),
        grid_spec=pltpu.PrefetchScalarGridSpec(
            num_scalar_prefetch=2, grid=(terms // GROUP,),
            in_specs=[whole((nq, nb, nc))] * parts + [pl.BlockSpec((GROUP, nk, nk), lambda g, o, s: (clamp(g, s), 0, 0))] + left_specs
            + [ANY] * (2 if resume else 1),
            out_specs=[ANY, ANY],
            scratch_shapes=[pltpu.VMEM((nq, nb, na), F32), pltpu.VMEM((nq, nb, parts * GROUP * nc), BF16),
                            pltpu.SemaphoreType.DMA, pltpu.SemaphoreType.DMA((2,))]),
        out_shape=[jax.ShapeDtypeStruct((nq, nb, na), F32), jax.ShapeDtypeStruct(carried.shape, carried.dtype)],
        input_output_aliases=aliases,
        compiler_params=pltpu.CompilerParams(dimension_semantics=('arbitrary',), vmem_limit_bytes=VMEM_LIMIT),
        cost_estimate=pl.CostEstimate(flops=n * 2 * nq * nb * parts * nc * (na + nk), bytes_accessed=n * na * nc * parts * 2, transcendentals=0),
        name='one_sided',
    )(order, split, *u_parts, pair_blk, *[left_parts[c] for c in range(parts) for _ in range(GROUP)], *([sigma] if resume else []), carried)


def full_call(order, split, u_part, right_slab, pair_blk, left_part, sigma, carried):
    nq, nb, na = sigma.shape
    nc = u_part.shape[-1]
    terms, _, nd = right_slab.shape
    nk = nq * ROW_TILE

    def at_least(g, s):
        return jnp.minimum(jnp.maximum(g, s[0]), terms // GROUP - 1)

    left_specs = [pl.BlockSpec((1, nc, na), functools.partial(lambda g, o, s, t: (o[at_least(g, s) * GROUP + t], 0, 0), t=t))
                  for t in range(GROUP)]
    n = terms // 2
    return pl.pallas_call(
        functools.partial(full_body, gathered=u_part.ndim == 4),
        grid_spec=pltpu.PrefetchScalarGridSpec(
            num_scalar_prefetch=2, grid=(terms // GROUP,),
            in_specs=[ANY,
                      pl.BlockSpec((GROUP, nb, nd), lambda g, o, s: (at_least(g, s), 0, 0)),
                      pl.BlockSpec((GROUP, nk, nk), lambda g, o, s: (at_least(g, s), 0, 0))] + left_specs + [ANY, ANY],
            out_specs=[ANY, ANY],
            scratch_shapes=[pltpu.VMEM((nq, nb, na), F32), pltpu.VMEM(u_part.shape, BF16),
                            pltpu.VMEM((nq, GROUP * nb, nc), BF16), pltpu.VMEM((nq, nb, GROUP * nc), BF16),
                            pltpu.SemaphoreType.DMA((nq,)), pltpu.SemaphoreType.DMA, pltpu.SemaphoreType.DMA((2,))]),
        out_shape=[jax.ShapeDtypeStruct((nq, nb, na), F32), jax.ShapeDtypeStruct(carried.shape, carried.dtype)],
        input_output_aliases={2 + 3 + GROUP: 0, 2 + 4 + GROUP: 1},
        compiler_params=pltpu.CompilerParams(dimension_semantics=('arbitrary',), vmem_limit_bytes=VMEM_LIMIT),
        cost_estimate=pl.CostEstimate(flops=n * 2 * nq * nb * nc * (nd + na + nk), bytes_accessed=n * na * nc * 2 + u_part.size * 2, transcendentals=0),
        name='full_terms',
    )(order, split, u_part, right_slab, pair_blk, *[left_part] * GROUP, sigma, carried)


def place_body(*refs, num, width):
    x_ref, out_ref = refs[0], refs[-1]
    for src in range(num):
        out_ref[0, :, :, src * width:(src + 1) * width] = x_ref[src]


def place_call(arrived, krylov, index):
    num, rows, nq, width = arrived.shape
    blk = rows // 4
    return pl.pallas_call(
        functools.partial(place_body, num=num, width=width),
        grid=(4,),
        in_specs=[pl.BlockSpec((num, blk, nq, width), lambda i: (0, i, 0, 0)), ANY],
        out_specs=pl.BlockSpec((1, blk, nq, num * width), lambda i: (index, i, 0, 0)),
        out_shape=jax.ShapeDtypeStruct(krylov.shape, krylov.dtype),
        input_output_aliases={1: 0},
        compiler_params=pltpu.CompilerParams(dimension_semantics=('arbitrary',), vmem_limit_bytes=VMEM_LIMIT),
        cost_estimate=pl.CostEstimate(flops=0, bytes_accessed=8 * arrived.size, transcendentals=0),
        name='place',
    )(arrived, krylov)


def first_body(me_ref, norm_ref, psi_ref, out_ref):
    out_ref[0] = psi_ref[...] / norm_ref[:1, :1]


def first_call(wavefunction, norm_tile, me, rows, count):
    _, nq, width = wavefunction.shape
    blk = rows // 4
    return pl.pallas_call(
        first_body,
        grid_spec=pltpu.PrefetchScalarGridSpec(
            num_scalar_prefetch=1, grid=(4,),
            in_specs=[pl.BlockSpec((8, 128), lambda i, m: (0, 0)), pl.BlockSpec((blk, nq, width), lambda i, m: (m[0] * 4 + i, 0, 0))],
            out_specs=pl.BlockSpec((1, blk, nq, width), lambda i, m: (0, i, 0, 0))),
        out_shape=jax.ShapeDtypeStruct((count, rows, nq, width), F32),
        compiler_params=pltpu.CompilerParams(dimension_semantics=('arbitrary',), vmem_limit_bytes=VMEM_LIMIT),
        cost_estimate=pl.CostEstimate(flops=rows * nq * width, bytes_accessed=8 * rows * nq * width, transcendentals=0),
        name='first',
    )(me, norm_tile, wavefunction)


def exchange_body(x_ref, out_ref, send_sem, recv_sem, *, num):
    me = lax.axis_index(AXIS_NAME)
    barrier = pltpu.get_barrier_semaphore()
    for off in range(1, num):
        pl.semaphore_signal(barrier, inc=1, device_id=(lax.rem(me + off, num),), device_id_type=pl.DeviceIdType.MESH)
    pl.semaphore_wait(barrier, num - 1)
    copies = []
    for off in range(1, num):
        copies.append(pltpu.make_async_remote_copy(
            src_ref=x_ref, dst_ref=out_ref.at[me], send_sem=send_sem.at[off - 1], recv_sem=recv_sem.at[off - 1],
            device_id=(lax.rem(me + off, num),), device_id_type=pl.DeviceIdType.MESH))
    for copy in copies:
        copy.start()
    out_ref[me] = x_ref[...]
    for copy in copies:
        copy.wait()


def exchange_call(x, num):
    vmem = pl.BlockSpec(memory_space=pltpu.VMEM)
    return pl.pallas_call(
        functools.partial(exchange_body, num=num), in_specs=[vmem], out_specs=vmem,
        out_shape=jax.ShapeDtypeStruct((num,) + x.shape, x.dtype),
        scratch_shapes=[pltpu.SemaphoreType.DMA((num - 1,))] * 2,
        compiler_params=pltpu.CompilerParams(collective_id=20, has_side_effects=True, vmem_limit_bytes=VMEM_LIMIT),
        name='exchange')(x)


def sum_over_devices(slot_ref, value, send_sem, recv_sem, me, num):
    slot_ref[me] = value
    copies = []
    for off in range(1, num):
        peer = lax.rem(me + off, num)
        copies.append(pltpu.make_async_remote_copy(
            src_ref=slot_ref.at[me], dst_ref=slot_ref.at[me], send_sem=send_sem.at[off - 1], recv_sem=recv_sem.at[off - 1],
            device_id=(peer,), device_id_type=pl.DeviceIdType.MESH))
    for copy in copies:
        copy.start()
    for copy in copies:
        copy.wait()
    total = slot_ref[0]
    for src in range(1, num):
        total = total + slot_ref[src]
    return jnp.sum(total)


def fold(prod):
    rows, cols = prod.shape
    part = jnp.sum(prod.reshape(rows // 8, 8, cols), axis=0)
    out = part[:, :128]
    for i in range(1, cols // 128):
        out = out + part[:, i * 128:(i + 1) * 128]
    return out


def finish_body(beta_prev_ref, sigma_hbm, cur_hbm, prev_hbm, next_hbm, u0, u1, u2, alpha_ref, beta_ref,
                sigma_ref, cur_ref, prev_ref, low_ref, slot_a, slot_b, in_sem, out_sem, send_a, recv_a, send_b, recv_b, *, num, vec_size):
    me = lax.axis_index(AXIS_NAME)
    nq, _, _ = sigma_ref.shape
    blk = nq // FIN_BLOCKS

    def load(n, i):
        src, dst = ((sigma_hbm, sigma_ref), (cur_hbm, cur_ref), (prev_hbm, prev_ref))[n]
        rows = pl.ds(i * blk, blk)
        return pltpu.make_async_copy(src.at[rows], dst.at[rows], in_sem.at[n, i])

    for i in range(FIN_BLOCKS):
        load(0, i).start()
        load(1, i).start()
    for i in range(FIN_BLOCKS):
        load(2, i).start()
    barrier = pltpu.get_barrier_semaphore()
    for off in range(1, num):
        pl.semaphore_signal(barrier, inc=1, device_id=(lax.rem(me + off, num),), device_id_type=pl.DeviceIdType.MESH)

    part = jnp.zeros((8, 128), F32)
    for i in range(FIN_BLOCKS):
        load(0, i).wait()
        load(1, i).wait()
        part = lax.fori_loop(i * blk, (i + 1) * blk, lambda q, acc: acc + fold(sigma_ref[q] * cur_ref[q]), part)
    pl.semaphore_wait(barrier, num - 1)
    alpha = sum_over_devices(slot_a, part, send_a, recv_a, me, num) / vec_size
    beta_prev = beta_prev_ref[0]
    for i in range(FIN_BLOCKS):
        load(2, i).wait()

    def residual_part(q, acc):
        res = sigma_ref[q] - alpha * cur_ref[q] - beta_prev * prev_ref[q]
        sigma_ref[q] = res
        return acc + fold(res * res)

    part = lax.fori_loop(0, nq, residual_part, jnp.zeros((8, 128), F32))
    norm = sum_over_devices(slot_b, part, send_b, recv_b, me, num) / vec_size
    beta_vec = jnp.sqrt(jnp.full((8, 128), norm, F32))
    alpha_ref[...] = jnp.full((8, 128), alpha, F32)
    beta_ref[...] = beta_vec
    beta_row = beta_vec[:1, :1]

    def scale_part(q, carry):
        nxt = sigma_ref[q] / beta_row
        cur_ref[q] = nxt
        low_ref[q] = nxt.astype(BF16)
        return carry

    def stores(i):
        rows = pl.ds(i * blk, blk)
        return [pltpu.make_async_copy(cur_ref.at[rows], next_hbm.at[rows], out_sem.at[0, i])] + [
            pltpu.make_async_copy(low_ref.at[rows, :, pl.ds(n * CHUNK, CHUNK)], ref.at[rows], out_sem.at[1 + n, i])
            for n, ref in enumerate((u0, u1, u2))]

    for i in range(FIN_BLOCKS):
        lax.fori_loop(i * blk, (i + 1) * blk, scale_part, 0)
        for copy in stores(i):
            copy.start()
    for i in range(FIN_BLOCKS):
        for copy in stores(i):
            copy.wait()


def finish_call(beta_prev, sigma, cur, prev, num, vec_size, call_id):
    nq, nb, na = sigma.shape
    vmem = pl.BlockSpec(memory_space=pltpu.VMEM)
    return pl.pallas_call(
        functools.partial(finish_body, num=num, vec_size=vec_size),
        in_specs=[pl.BlockSpec(memory_space=pltpu.SMEM)] + [ANY] * 3,
        out_specs=[ANY] * 4 + [vmem] * 2,
        out_shape=[jax.ShapeDtypeStruct((nq, nb, na), F32)] + [jax.ShapeDtypeStruct((nq, nb, CHUNK), BF16)] * 3
        + [jax.ShapeDtypeStruct((8, 128), F32)] * 2,
        scratch_shapes=[pltpu.VMEM((nq, nb, na), F32)] * 3 + [pltpu.VMEM((nq, nb, na), BF16)] + [pltpu.VMEM((num, 8, 128), F32)] * 2
        + [pltpu.SemaphoreType.DMA((3, FIN_BLOCKS)), pltpu.SemaphoreType.DMA((4, FIN_BLOCKS))] + [pltpu.SemaphoreType.DMA((num - 1,))] * 4,
        compiler_params=pltpu.CompilerParams(collective_id=call_id, has_side_effects=True, vmem_limit_bytes=VMEM_LIMIT),
        cost_estimate=pl.CostEstimate(flops=10 * sigma.size, bytes_accessed=22 * sigma.size, transcendentals=0),
        name='finish',
    )(beta_prev, sigma, cur, prev)


def solution(mesh):
    num = mesh.shape[AXIS_NAME]

    def device_body(wavefunction, left_loc, pair_loc, right_loc, flag_loc):
        bond, nq, _ = wavefunction.shape
        vec_size = wavefunction.size
        slab = bond // num
        me = lax.axis_index(AXIS_NAME)
        nchunk = bond // CHUNK

        terms_loc = pair_loc.shape[0]
        small = jnp.concatenate([pair_loc.astype(F32).reshape(8, 128), jnp.pad(flag_loc.astype(F32), (0, 1024 - terms_loc)).reshape(8, 128)])
        small_all = exchange_call(small, num)
        right_slab = lax.all_to_all(right_loc, AXIS_NAME, split_axis=1, concat_axis=0, tiled=True)
        left_parts = []
        for i in range(nchunk):
            left_parts.append(lax.all_gather(left_loc[:, i * CHUNK:(i + 1) * CHUNK], AXIS_NAME, axis=0, tiled=True))
        pair_all = small_all[:, :8].reshape(num * terms_loc, nq, nq).astype(BF16)
        flags = small_all[:, 8, :terms_loc].reshape(-1).astype(jnp.int32)
        order = jnp.argsort(flags, stable=True).astype(jnp.int32)
        split = ((flags.shape[0] - jnp.sum(flags)) // GROUP).astype(jnp.int32).reshape(1)
        unit = (jnp.arange(slab)[:, None] + me * slab == jnp.arange(bond)[None, :]).astype(BF16)
        right_slab = jnp.where(flags[:, None, None] == 1, right_slab, unit[None])[order]
        eye = jnp.eye(ROW_TILE, dtype=BF16)
        pair_sorted = pair_all[order]
        pair_blk = (pair_sorted[:, :, None, :, None] * eye[None, None, :, None, :]).reshape(-1, nq * ROW_TILE, nq * ROW_TILE)

        norm0 = jnp.sqrt(jnp.sum(wavefunction * wavefunction) / vec_size)
        krylov = first_call(wavefunction, jnp.full((8, 128), norm0, F32), me.reshape(1).astype(jnp.int32), slab, LANCZOS_STEPS + 1)
        cur = (lax.dynamic_slice_in_dim(wavefunction, me * slab, slab, axis=2) / norm0).transpose(1, 2, 0)
        cur_low = cur.astype(BF16)
        u_parts = [cur_low[:, :, i * CHUNK:(i + 1) * CHUNK] for i in range(nchunk)]
        whole_low = (wavefunction / norm0).astype(BF16).transpose(1, 2, 0)
        u_wide = [whole_low[:, :, i * CHUNK:(i + 1) * CHUNK] for i in range(nchunk)]
        prev = jnp.zeros_like(cur)
        beta_prev = jnp.zeros((1,), F32)
        tiles = []
        leaving = arriving = None
        for step in range(LANCZOS_STEPS):
            if step == 0:
                sigma = None
                for i in range(nchunk):
                    sigma, krylov = one_sided_call(order, split, u_parts[i:i + 1], pair_blk, left_parts[i:i + 1], krylov, sigma)
                    sigma, krylov = full_call(order, split, u_wide[i], right_slab, pair_blk, left_parts[i], sigma, krylov)
            else:
                if arriving is None:
                    sigma, krylov = one_sided_call(order, split, u_parts, pair_blk, left_parts, krylov)
                else:
                    sigma, arriving = one_sided_call(order, split, u_parts, pair_blk, left_parts, arriving)
                    krylov = place_call(arriving, krylov, step - 1)
                sigma, krylov = full_call(order, split, u_wide[0], right_slab, pair_blk, left_parts[0], sigma, krylov)
                sigma, leaving = full_call(order, split, u_wide[1], right_slab, pair_blk, left_parts[1], sigma, leaving)
                arriving = lax.all_to_all(leaving, AXIS_NAME, split_axis=0, concat_axis=0, tiled=False)
                sigma, krylov = full_call(order, split, u_wide[2], right_slab, pair_blk, left_parts[2], sigma, krylov)
            nxt, *u_parts, alpha_t, beta_t = finish_call(beta_prev, sigma, cur, prev, num, vec_size, step)
            beta_prev = beta_t[0, :1]
            tiles += [alpha_t[0, :1], beta_prev]
            if step + 1 < LANCZOS_STEPS:
                u_wide = [lax.all_gather(part, AXIS_NAME, axis=0, tiled=False) for part in u_parts]
            prev, cur = cur, nxt
            leaving = nxt.transpose(2, 0, 1).reshape(num, slab, nq, slab)
        krylov = place_call(arriving, krylov, LANCZOS_STEPS - 1)
        arriving = lax.all_to_all(leaving, AXIS_NAME, split_axis=0, concat_axis=0, tiled=False)
        krylov = place_call(arriving, krylov, LANCZOS_STEPS)
        scalars = jnp.concatenate(tiles)
        return krylov, scalars[0::2], scalars[1::2]

    return jax.shard_map(device_body, mesh=mesh, in_specs=(P(), P(AXIS_NAME), P(AXIS_NAME), P(AXIS_NAME), P(AXIS_NAME)), out_specs=(P(None, AXIS_NAME), P(), P()), check_vma=False)
```

profile of v0, /device:TPU:0, one launch (start us, length us, event | category | flops | bytes accessed | tf_op | source)
XLA Modules:
  0.0 1799.1 jit_solution(4068996797585379130)
XLA Ops:
  7.2 4.6 fusion.5
  13.3 8.2 copy.90
  21.5 4.3 all-to-all-start
  26.8 87.3 %exchange.1 = f32[8,16,128]{2,1,0:T(8,128)} custom-call(f32[16,128]{1,0:T(8,128)} %pad_maximum_fusion.x_ref), custom_call_target="tpu_custom_call" | custom-call | tf_op jit(solution)/shard_map/exchange/pallas_call | solution.py:269
  119.6 6.4 mul.29
  125.9 16.6 copy.94
  143.7 37.0 %copy.89 = f32[768,16,768]{0,2,1:T(8,128)} copy(f32[768,16,768]{2,1,0:T(8,128)} %psi_ref.1) | data formatting | bytes 75497472 | tf_op args[0]
  180.7 17.6 multiply_reduce_fusion
  199.7 5.3 first.1.rest_6_
  205.1 5.4 fusion.3
  214.2 15.4 fusion
  229.7 7.0 fusion.4
  243.0 5.5 gather_fusion
  248.5 19.6 %one_sided.8 = (f32[16,96,768]{2,1,0:T(8,128)}, f32[7,96,16,768]{3,2,1,0:T(8,128)}) custom-call(s32[32]{0:T(128)} %copy-done.1, s32[1]{0:T(128)} %bitcast.1.split_ref, bf16[16,96,256]{2,1,0:T(8,128)(2,1)} %get-tuple-element.185.rest_0_, bf16[32,256,256]{2,1,0:T(8,128)(2,1)} %broadcast_multiply_fusion.rest_1_.pair_ref.rest_3_, ...), custom_call_target="tpu_custom_call", output_to_operand_aliasing={{1}: (8, {})} | custom-call | flops 12884901888 | bytes 6291456 | tf_op jit(solution)/shard_map/one_sided/pallas_call | solution.py:159
  268.1 32.4 %full_terms.18 = (f32[16,96,768]{2,1,0:T(8,128)}, f32[7,96,16,768]{3,2,1,0:T(8,128)}) custom-call(s32[32]{0:T(128)} %copy-done.1, s32[1]{0:T(128)} %bitcast.1.split_ref, bf16[16,768,256]{2,1,0:T(8,128)(2,1)} %get-tuple-element.179.u_hbm, bf16[32,96,768]{2,1,0:T(8,128)(2,1)} %gather_fusion, ...), custom_call_target="tpu_custom_call", output_to_operand_aliasing={{0}: (9, {}), {1}: (10, {})} | custom-call | flops 22548578304 | bytes 12582912 | tf_op jit(solution)/shard_map/full_terms/pallas_call | solution.py:188
  300.5 21.8 %one_sided.9 = (f32[16,96,768]{2,1,0:T(8,128)}, f32[7,96,16,768]{3,2,1,0:T(8,128)}) custom-call(s32[32]{0:T(128)} %copy-done.1, s32[1]{0:T(128)} %bitcast.1.split_ref, bf16[16,96,256]{2,1,0:T(8,128)(2,1)} %get-tuple-element.186.rest_0_, ...), custom_call_target="tpu_custom_call", output_to_operand_aliasing={{0}: (8, {}), {1}: (9, {})} | custom-call | flops 12884901888 | bytes 6291456 | tf_op jit(solution)/shard_map/one_sided/pallas_call | solution.py:159
  322.3 32.6 %full_terms.19 = (f32[16,96,768]{2,1,0:T(8,128)}, f32[7,96,16,768]{3,2,1,0:T(8,128)}) custom-call(s32[32]{0:T(128)} %copy-done.1, s32[1]{0:T(128)} %bitcast.1.split_ref, bf16[16,768,256]{2,1,0:T(8,128)(2,1)} %get-tuple-element.180.u_hbm, bf16[32,96,768]{2,1,0:T(8,128)(2,1)} %gather_fusion, ...), custom_call_target="tpu_custom_call", output_to_operand_aliasing={{0}: (9, {}), {1}: (10, {})} | custom-call | flops 22548578304 | bytes 12582912 | tf_op jit(solution)/shard_map/full_terms/pallas_call | solution.py:188
  354.9 21.8 %one_sided.10 = (f32[16,96,768]{2,1,0:T(8,128)}, f32[7,96,16,768]{3,2,1,0:T(8,128)}) custom-call(s32[32]{0:T(128)} %copy-done.1, s32[1]{0:T(128)} %bitcast.1.split_ref, bf16[16,96,256]{2,1,0:T(8,128)(2,1)} %get-tuple-element.187.rest_0_, ...), custom_call_target="tpu_custom_call", output_to_operand_aliasing={{0}: (8, {}), {1}: (9, {})} | custom-call | flops 12884901888 | bytes 6291456 | tf_op jit(solution)/shard_map/one_sided/pallas_call | solution.py:159
  376.7 32.3 %full_terms.20 = (f32[16,96,768]{2,1,0:T(8,128)}, f32[7,96,16,768]{3,2,1,0:T(8,128)}) custom-call(s32[32]{0:T(128)} %copy-done.1, s32[1]{0:T(128)} %bitcast.1.split_ref, bf16[16,768,256]{2,1,0:T(8,128)(2,1)} %get-tuple-element.181.u_hbm, bf16[32,96,768]{2,1,0:T(8,128)(2,1)} %gather_fusion, ...), custom_call_target="tpu_custom_call", output_to_operand_aliasing={{0}: (9, {}), {1}: (10, {})} | custom-call | flops 22548578304 | bytes 12582912 | tf_op jit(solution)/shard_map/full_terms/pallas_call | solution.py:188
  411.7 15.5 finish.6
  428.5 6.6 copy.96
  436.3 47.6 %one_sided.11 = (f32[16,96,768]{2,1,0:T(8,128)}, f32[7,96,16,768]{3,2,1,0:T(8,128)}) custom-call(s32[32]{0:T(128)} %copy-done.1, s32[1]{0:T(128)} %bitcast.1.split_ref, bf16[16,96,256]{2,1,0:T(8,128)(2,1)} %get-tuple-element.104.rest_0_, bf16[16,96,256]{2,1,0:T(8,128)(2,1)} %get-tuple-element.103.rest_1_, ...), custom_call_target="tpu_custom_call", output_to_operand_aliasing={{1}: (18, {})} | custom-call | flops 38654705664 | bytes 18874368 | tf_op jit(solution)/shard_map/one_sided/pallas_call | solution.py:159
  483.9 33.4 %full_terms.21 = (f32[16,96,768]{2,1,0:T(8,128)}, f32[7,96,16,768]{3,2,1,0:T(8,128)}) custom-call(s32[32]{0:T(128)} %copy-done.1, s32[1]{0:T(128)} %bitcast.1.split_ref, bf16[8,16,96,256]{3,2,1,0:T(8,128)(2,1)} %bitcast.78, bf16[32,96,768]{2,1,0:T(8,128)(2,1)} %gather_fusion, ...), custom_call_target="tpu_custom_call", output_to_operand_aliasing={{0}: (9, {}), {1}: (10, {})} | custom-call | flops 22548578304 | bytes 12582912 | tf_op jit(solution)/shard_map/full_terms/pallas_call | solution.py:188
  517.4 32.1 %full_terms.22 = (f32[16,96,768]{2,1,0:T(8,128)}, f32[8,96,16,96]{3,2,1,0:T(8,128)}) custom-call(s32[32]{0:T(128)} %copy-done.1, s32[1]{0:T(128)} %bitcast.1.split_ref, bf16[8,16,96,256]{3,2,1,0:T(8,128)(2,1)} %bitcast.84, bf16[32,96,768]{2,1,0:T(8,128)(2,1)} %gather_fusion, ...), custom_call_target="tpu_custom_call", output_to_operand_aliasing={{0}: (9, {}), {1}: (10, {})} | custom-call | flops 22548578304 | bytes 12582912 | tf_op jit(solution)/shard_map/full_terms/pallas_call | solution.py:188
  549.9 32.6 %full_terms.23 = (f32[16,96,768]{2,1,0:T(8,128)}, f32[7,96,16,768]{3,2,1,0:T(8,128)}) custom-call(s32[32]{0:T(128)} %copy-done.1, s32[1]{0:T(128)} %bitcast.1.split_ref, bf16[8,16,96,256]{3,2,1,0:T(8,128)(2,1)} %bitcast.77, bf16[32,96,768]{2,1,0:T(8,128)(2,1)} %gather_fusion, ...), custom_call_target="tpu_custom_call", output_to_operand_aliasing={{0}: (9, {}), {1}: (10, {})} | custom-call | flops 22548578304 | bytes 12582912 | tf_op jit(solution)/shard_map/full_terms/pallas_call | solution.py:188
  582.5 16.2 finish.7
  603.8 6.5 copy.97
  611.4 88.4 %all-to-all-done.1.rest_16_ = f32[8,96,16,96]{3,2,1,0:T(8,128)} async-done(((f32[8,96,16,96]{3,2,1,0:T(8,128)}), f32[8,96,16,96]{3,2,1,0:T(8,128)}, u32[]{:S(2)}, u32[]{:S(2)}) %all-to-all-start.1) | async-done | bytes 4718624 | tf_op jit(solution)/shard_map/all_to_all | solution.py:437
  699.8 48.0 %one_sided.12 = (f32[16,96,768]{2,1,0:T(8,128)}, f32[8,96,16,96]{3,2,1,0:T(8,128)}) custom-call(s32[32]{0:T(128)} %copy-done.1, s32[1]{0:T(128)} %bitcast.1.split_ref, bf16[16,96,256]{2,1,0:T(8,128)(2,1)} %get-tuple-element.116.rest_0_, bf16[16,96,256]{2,1,0:T(8,128)(2,1)} %get-tuple-element.115.rest_1_, ...), custom_call_target="tpu_custom_call", output_to_operand_aliasing={{1}: (18, {})} | custom-call | flops 38654705664 | bytes 18874368 | tf_op jit(solution)/shard_map/one_sided/pallas_call | solution.py:159
  747.8 6.0 place.6.rest_5_
  753.8 32.3 %full_terms.24 = (f32[16,96,768]{2,1,0:T(8,128)}, f32[7,96,16,768]{3,2,1,0:T(8,128)}) custom-call(s32[32]{0:T(128)} %copy-done.1, s32[1]{0:T(128)} %bitcast.1.split_ref, bf16[8,16,96,256]{3,2,1,0:T(8,128)(2,1)} %bitcast.70, bf16[32,96,768]{2,1,0:T(8,128)(2,1)} %gather_fusion, ...), custom_call_target="tpu_custom_call", output_to_operand_aliasing={{0}: (9, {}), {1}: (10, {})} | custom-call | flops 22548578304 | bytes 12582912 | tf_op jit(solution)/shard_map/full_terms/pallas_call | solution.py:188
  786.1 32.1 %full_terms.25 = (f32[16,96,768]{2,1,0:T(8,128)}, f32[8,96,16,96]{3,2,1,0:T(8,128)}) custom-call(s32[32]{0:T(128)} %copy-done.1, s32[1]{0:T(128)} %bitcast.1.split_ref, bf16[8,16,96,256]{3,2,1,0:T(8,128)(2,1)} %bitcast.80, bf16[32,96,768]{2,1,0:T(8,128)(2,1)} %gather_fusion, ...), custom_call_target="tpu_custom_call", output_to_operand_aliasing={{0}: (9, {}), {1}: (10, {})} | custom-call | flops 22548578304 | bytes 12582912 | tf_op jit(solution)/shard_map/full_terms/pallas_call | solution.py:188
  818.3 32.4 %full_terms.26 = (f32[16,96,768]{2,1,0:T(8,128)}, f32[7,96,16,768]{3,2,1,0:T(8,128)}) custom-call(s32[32]{0:T(128)} %copy-done.1, s32[1]{0:T(128)} %bitcast.1.split_ref, bf16[8,16,96,256]{3,2,1,0:T(8,128)(2,1)} %bitcast.74, bf16[32,96,768]{2,1,0:T(8,128)(2,1)} %gather_fusion, ...), custom_call_target="tpu_custom_call", output_to_operand_aliasing={{0}: (9, {}), {1}: (10, {})} | custom-call | flops 22548578304 | bytes 12582912 | tf_op jit(solution)/shard_map/full_terms/pallas_call | solution.py:188
  850.7 16.1 finish.8
  871.7 6.8 copy.98
  879.8 87.6 %all-to-all-done.2.rest_16_ = f32[8,96,16,96]{3,2,1,0:T(8,128)} async-done(((f32[8,96,16,96]{3,2,1,0:T(8,128)}), f32[8,96,16,96]{3,2,1,0:T(8,128)}, u32[]{:S(2)}, u32[]{:S(2)}) %all-to-all-start.2) | async-done | bytes 4718624 | tf_op jit(solution)/shard_map/all_to_all | solution.py:437
  967.4 47.9 %one_sided.13 = (f32[16,96,768]{2,1,0:T(8,128)}, f32[8,96,16,96]{3,2,1,0:T(8,128)}) custom-call(s32[32]{0:T(128)} %copy-done.1, s32[1]{0:T(128)} %bitcast.1.split_ref, bf16[16,96,256]{2,1,0:T(8,128)(2,1)} %get-tuple-element.129.rest_0_, bf16[16,96,256]{2,1,0:T(8,128)(2,1)} %get-tuple-element.128.rest_1_, ...), custom_call_target="tpu_custom_call", output_to_operand_aliasing={{1}: (18, {})} | custom-call | flops 38654705664 | bytes 18874368 | tf_op jit(solution)/shard_map/one_sided/pallas_call | solution.py:159
  1015.3 6.0 place.7.rest_5_
  1021.2 32.3 %full_terms.27 = (f32[16,96,768]{2,1,0:T(8,128)}, f32[7,96,16,768]{3,2,1,0:T(8,128)}) custom-call(s32[32]{0:T(128)} %copy-done.1, s32[1]{0:T(128)} %bitcast.1.split_ref, bf16[8,16,96,256]{3,2,1,0:T(8,128)(2,1)} %bitcast.71, bf16[32,96,768]{2,1,0:T(8,128)(2,1)} %gather_fusion, ...), custom_call_target="tpu_custom_call", output_to_operand_aliasing={{0}: (9, {}), {1}: (10, {})} | custom-call | flops 22548578304 | bytes 12582912 | tf_op jit(solution)/shard_map/full_terms/pallas_call | solution.py:188
  1053.5 32.1 %full_terms.28 = (f32[16,96,768]{2,1,0:T(8,128)}, f32[8,96,16,96]{3,2,1,0:T(8,128)}) custom-call(s32[32]{0:T(128)} %copy-done.1, s32[1]{0:T(128)} %bitcast.1.split_ref, bf16[8,16,96,256]{3,2,1,0:T(8,128)(2,1)} %bitcast.81, bf16[32,96,768]{2,1,0:T(8,128)(2,1)} %gather_fusion, ...), custom_call_target="tpu_custom_call", output_to_operand_aliasing={{0}: (9, {}), {1}: (10, {})} | custom-call | flops 22548578304 | bytes 12582912 | tf_op jit(solution)/shard_map/full_terms/pallas_call | solution.py:188
  1085.7 32.3 %full_terms.29 = (f32[16,96,768]{2,1,0:T(8,128)}, f32[7,96,16,768]{3,2,1,0:T(8,128)}) custom-call(s32[32]{0:T(128)} %copy-done.1, s32[1]{0:T(128)} %bitcast.1.split_ref, bf16[8,16,96,256]{3,2,1,0:T(8,128)(2,1)} %bitcast.75, bf16[32,96,768]{2,1,0:T(8,128)(2,1)} %gather_fusion, ...), custom_call_target="tpu_custom_call", output_to_operand_aliasing={{0}: (9, {}), {1}: (10, {})} | custom-call | flops 22548578304 | bytes 12582912 | tf_op jit(solution)/shard_map/full_terms/pallas_call | solution.py:188
  1118.1 16.2 finish.9
  1139.1 6.7 copy.99
  1147.0 88.1 %all-to-all-done.3.rest_16_ = f32[8,96,16,96]{3,2,1,0:T(8,128)} async-done(((f32[8,96,16,96]{3,2,1,0:T(8,128)}), f32[8,96,16,96]{3,2,1,0:T(8,128)}, u32[]{:S(2)}, u32[]{:S(2)}) %all-to-all-start.3) | async-done | bytes 4718624 | tf_op jit(solution)/shard_map/all_to_all | solution.py:437
  1235.1 48.0 %one_sided.14 = (f32[16,96,768]{2,1,0:T(8,128)}, f32[8,96,16,96]{3,2,1,0:T(8,128)}) custom-call(s32[32]{0:T(128)} %copy-done.1, s32[1]{0:T(128)} %bitcast.1.split_ref, bf16[16,96,256]{2,1,0:T(8,128)(2,1)} %get-tuple-element.142.rest_0_, bf16[16,96,256]{2,1,0:T(8,128)(2,1)} %get-tuple-element.141.rest_1_, ...), custom_call_target="tpu_custom_call", output_to_operand_aliasing={{1}: (18, {})} | custom-call | flops 38654705664 | bytes 18874368 | tf_op jit(solution)/shard_map/one_sided/pallas_call | solution.py:159
  1283.1 6.0 place.8.rest_5_
  1289.1 32.6 %full_terms.30 = (f32[16,96,768]{2,1,0:T(8,128)}, f32[7,96,16,768]{3,2,1,0:T(8,128)}) custom-call(s32[32]{0:T(128)} %copy-done.1, s32[1]{0:T(128)} %bitcast.1.split_ref, bf16[8,16,96,256]{3,2,1,0:T(8,128)(2,1)} %bitcast.72, bf16[32,96,768]{2,1,0:T(8,128)(2,1)} %gather_fusion, ...), custom_call_target="tpu_custom_call", output_to_operand_aliasing={{0}: (9, {}), {1}: (10, {})} | custom-call | flops 22548578304 | bytes 12582912 | tf_op jit(solution)/shard_map/full_terms/pallas_call | solution.py:188
  1321.7 32.1 %full_terms.31 = (f32[16,96,768]{2,1,0:T(8,128)}, f32[8,96,16,96]{3,2,1,0:T(8,128)}) custom-call(s32[32]{0:T(128)} %copy-done.1, s32[1]{0:T(128)} %bitcast.1.split_ref, bf16[8,16,96,256]{3,2,1,0:T(8,128)(2,1)} %bitcast.82, bf16[32,96,768]{2,1,0:T(8,128)(2,1)} %gather_fusion, ...), custom_call_target="tpu_custom_call", output_to_operand_aliasing={{0}: (9, {}), {1}: (10, {})} | custom-call | flops 22548578304 | bytes 12582912 | tf_op jit(solution)/shard_map/full_terms/pallas_call | solution.py:188
  1353.9 32.3 %full_terms.32 = (f32[16,96,768]{2,1,0:T(8,128)}, f32[7,96,16,768]{3,2,1,0:T(8,128)}) custom-call(s32[32]{0:T(128)} %copy-done.1, s32[1]{0:T(128)} %bitcast.1.split_ref, bf16[8,16,96,256]{3,2,1,0:T(8,128)(2,1)} %bitcast.76, bf16[32,96,768]{2,1,0:T(8,128)(2,1)} %gather_fusion, ...), custom_call_target="tpu_custom_call", output_to_operand_aliasing={{0}: (9, {}), {1}: (10, {})} | custom-call | flops 22548578304 | bytes 12582912 | tf_op jit(solution)/shard_map/full_terms/pallas_call | solution.py:188
  1386.2 16.0 finish.10
  1406.9 6.7 copy.100
  1413.6 89.2 %all-to-all-done.4.rest_16_ = f32[8,96,16,96]{3,2,1,0:T(8,128)} async-done(((f32[8,96,16,96]{3,2,1,0:T(8,128)}), f32[8,96,16,96]{3,2,1,0:T(8,128)}, u32[]{:S(2)}, u32[]{:S(2)}) %all-to-all-start.4) | async-done | bytes 4718624 | tf_op jit(solution)/shard_map/all_to_all | solution.py:437
  1502.8 47.9 %one_sided.15 = (f32[16,96,768]{2,1,0:T(8,128)}, f32[8,96,16,96]{3,2,1,0:T(8,128)}) custom-call(s32[32]{0:T(128)} %copy-done.1, s32[1]{0:T(128)} %bitcast.1.split_ref, bf16[16,96,256]{2,1,0:T(8,128)(2,1)} %get-tuple-element.155.rest_0_, bf16[16,96,256]{2,1,0:T(8,128)(2,1)} %get-tuple-element.154.rest_1_, ...), custom_call_target="tpu_custom_call", output_to_operand_aliasing={{1}: (18, {})} | custom-call | flops 38654705664 | bytes 18874368 | tf_op jit(solution)/shard_map/one_sided/pallas_call | solution.py:159
  1550.7 6.0 place.9.rest_5_
  1556.7 32.4 %full_terms.33 = (f32[16,96,768]{2,1,0:T(8,128)}, f32[7,96,16,768]{3,2,1,0:T(8,128)}) custom-call(s32[32]{0:T(128)} %copy-done.1, s32[1]{0:T(128)} %bitcast.1.split_ref, bf16[8,16,96,256]{3,2,1,0:T(8,128)(2,1)} %bitcast.73, bf16[32,96,768]{2,1,0:T(8,128)(2,1)} %gather_fusion, ...), custom_call_target="tpu_custom_call", output_to_operand_aliasing={{0}: (9, {}), {1}: (10, {})} | custom-call | flops 22548578304 | bytes 12582912 | tf_op jit(solution)/shard_map/full_terms/pallas_call | solution.py:188
  1589.1 32.1 %full_terms.34 = (f32[16,96,768]{2,1,0:T(8,128)}, f32[8,96,16,96]{3,2,1,0:T(8,128)}) custom-call(s32[32]{0:T(128)} %copy-done.1, s32[1]{0:T(128)} %bitcast.1.split_ref, bf16[8,16,96,256]{3,2,1,0:T(8,128)(2,1)} %bitcast.83, bf16[32,96,768]{2,1,0:T(8,128)(2,1)} %gather_fusion, ...), custom_call_target="tpu_custom_call", output_to_operand_aliasing={{0}: (9, {}), {1}: (10, {})} | custom-call | flops 22548578304 | bytes 12582912 | tf_op jit(solution)/shard_map/full_terms/pallas_call | solution.py:188
  1621.2 3.8 all-to-all-start.6
  1626.2 32.1 %full_terms.35 = (f32[16,96,768]{2,1,0:T(8,128)}, f32[7,96,16,768]{3,2,1,0:T(8,128)}) custom-call(s32[32]{0:T(128)} %copy-done.1, s32[1]{0:T(128)} %bitcast.1.split_ref, bf16[8,16,96,256]{3,2,1,0:T(8,128)(2,1)} %bitcast.69, bf16[32,96,768]{2,1,0:T(8,128)(2,1)} %gather_fusion, ...), custom_call_target="tpu_custom_call", output_to_operand_aliasing={{0}: (9, {}), {1}: (10, {})} | custom-call | flops 22548578304 | bytes 12582912 | tf_op jit(solution)/shard_map/full_terms/pallas_call | solution.py:188
  1658.3 46.2 %finish.11 = (f32[16,96,768]{2,1,0:T(8,128)}, bf16[16,96,256]{2,1,0:T(8,128)(2,1)}, bf16[16,96,256]{2,1,0:T(8,128)(2,1)}, bf16[16,96,256]{2,1,0:T(8,128)(2,1)}, f32[8,128]{1,0:T(8,128)}, /*index=5*/f32[8,128]{1,0:T(8,128)}) custom-call(f32[1]{0:T(128)} %bitcast.33.beta_prev_ref, f32[16,96,768]{2,1,0:T(8,128)} %get-tuple-element.164.sigma_hbm, ...), custom_call_target="tpu_custom_call" | custom-call | flops 11796480 | bytes 25952256 | tf_op jit(solution)/shard_map/finish/pallas_call | solution.py:371
  1704.4 6.3 copy.101
  1722.8 7.6 concatenate.7
  1731.6 5.9 place.10.refs_1_
  1737.5 48.3 %all-to-all-done.5.refs_0_ = f32[8,96,16,96]{3,2,1,0:T(8,128)} async-done(((f32[8,96,16,96]{3,2,1,0:T(8,128)}), f32[8,96,16,96]{3,2,1,0:T(8,128)}, u32[]{:S(2)}, u32[]{:S(2)}) %all-to-all-start.5) | async-done | bytes 4718624 | tf_op jit(solution)/shard_map/all_to_all | solution.py:447
  1785.8 5.9 place.11
  (110 shorter events, 62.1 us)
Async XLA Ops:
  7.2 241.3 %all-gather.38.cloned.1.call-start = ((), (), s32[]{:S(2)}) async-start(), calls=%async_computation.9 | async-start | bytes 14155776 | tf_op jit(solution)/shard_map/all_gather | solution.py:401
  11.9 288.6 %all-gather.36.cloned.1.call-start = ((), (), s32[]{:S(2)}) async-start(), calls=%async_computation.8 | async-start | bytes 14155776 | tf_op jit(solution)/shard_map/all_gather | solution.py:401
  12.6 342.3 %all-gather.34.cloned.1.call-start = ((), (), s32[]{:S(2)}) async-start(), calls=%async_computation.7 | async-start | bytes 14155776 | tf_op jit(solution)/shard_map/all_gather | solution.py:401
  21.5 4.5 copy-start.3
  21.5 4.6 copy-start.2
  21.5 215.1 %all-to-all-start = ((bf16[4,768,768]{2,0,1:T(4,128)(2,1)}), bf16[4,768,768]{2,0,1:T(4,128)(2,1)}, u32[]{:S(2)}, u32[]{:S(2)}) async-start(bf16[4,768,768]{2,0,1:T(4,128)(2,1)} %copy.90), calls=%async_computation | async-start | bytes 9437184 | tf_op jit(solution)/shard_map/all_to_all | solution.py:398
  25.8 458.1 %all-gather.44.cloned.1.call-start = ((), (), s32[]{:S(2)}) async-start(), calls=%async_computation.12 | async-start | bytes 7077888 | tf_op jit(solution)/shard_map/all_gather | solution.py:443
  118.8 7.1 copy-start.1
  205.1 6.8 copy-start
  427.2 90.1 %all-gather.42.cloned.1.call-start = ((), (), s32[]{:S(2)}) async-start(), calls=%async_computation.11 | async-start | bytes 7077888 | tf_op jit(solution)/shard_map/all_gather | solution.py:443
  427.8 122.1 %all-gather.40.cloned.1.call-start = ((), (), s32[]{:S(2)}) async-start(), calls=%async_computation.10 | async-start | bytes 7077888 | tf_op jit(solution)/shard_map/all_gather | solution.py:443
  428.4 325.4 %all-gather.50.cloned.1.call-start = ((), (), s32[]{:S(2)}) async-start(), calls=%async_computation.15 | async-start | bytes 7077888 | tf_op jit(solution)/shard_map/all_gather | solution.py:443
  598.7 187.4 %all-gather.48.cloned.1.call-start = ((), (), s32[]{:S(2)}) async-start(), calls=%async_computation.14 | async-start | bytes 7077888 | tf_op jit(solution)/shard_map/all_gather | solution.py:443
  599.4 100.4 %all-to-all-start.1 = ((f32[8,96,16,96]{3,2,1,0:T(8,128)}), f32[8,96,16,96]{3,2,1,0:T(8,128)}, u32[]{:S(2)}, u32[]{:S(2)}) async-start(f32[8,96,16,96]{3,2,1,0:T(8,128)} %get-tuple-element.117), calls=%async_computation.1 | async-start | bytes 12582912 | tf_op jit(solution)/shard_map/all_to_all | solution.py:437
  603.0 215.3 %all-gather.46.cloned.1.call-start = ((), (), s32[]{:S(2)}) async-start(), calls=%async_computation.13 | async-start | bytes 7077888 | tf_op jit(solution)/shard_map/all_gather | solution.py:443
  603.7 417.5 %all-gather.56.cloned.1.call-start = ((), (), s32[]{:S(2)}) async-start(), calls=%async_computation.18 | async-start | bytes 7077888 | tf_op jit(solution)/shard_map/all_gather | solution.py:443
  866.8 186.7 %all-gather.54.cloned.1.call-start = ((), (), s32[]{:S(2)}) async-start(), calls=%async_computation.17 | async-start | bytes 7077888 | tf_op jit(solution)/shard_map/all_gather | solution.py:443
  867.6 99.8 %all-to-all-start.2 = ((f32[8,96,16,96]{3,2,1,0:T(8,128)}), f32[8,96,16,96]{3,2,1,0:T(8,128)}, u32[]{:S(2)}, u32[]{:S(2)}) async-start(f32[8,96,16,96]{3,2,1,0:T(8,128)} %get-tuple-element.130), calls=%async_computation.2 | async-start | bytes 12582912 | tf_op jit(solution)/shard_map/all_to_all | solution.py:437
  871.1 214.6 %all-gather.52.cloned.1.call-start = ((), (), s32[]{:S(2)}) async-start(), calls=%async_computation.16 | async-start | bytes 7077888 | tf_op jit(solution)/shard_map/all_gather | solution.py:443
  871.7 417.4 %all-gather.62.cloned.1.call-start = ((), (), s32[]{:S(2)}) async-start(), calls=%async_computation.21 | async-start | bytes 7077888 | tf_op jit(solution)/shard_map/all_gather | solution.py:443
  1134.3 187.4 %all-gather.60.cloned.1.call-start = ((), (), s32[]{:S(2)}) async-start(), calls=%async_computation.20 | async-start | bytes 7077888 | tf_op jit(solution)/shard_map/all_gather | solution.py:443
  1134.9 100.2 %all-to-all-start.3 = ((f32[8,96,16,96]{3,2,1,0:T(8,128)}), f32[8,96,16,96]{3,2,1,0:T(8,128)}, u32[]{:S(2)}, u32[]{:S(2)}) async-start(f32[8,96,16,96]{3,2,1,0:T(8,128)} %get-tuple-element.143), calls=%async_computation.3 | async-start | bytes 12582912 | tf_op jit(solution)/shard_map/all_to_all | solution.py:437
  1138.4 215.4 %all-gather.58.cloned.1.call-start = ((), (), s32[]{:S(2)}) async-start(), calls=%async_computation.19 | async-start | bytes 7077888 | tf_op jit(solution)/shard_map/all_gather | solution.py:443
  1139.0 417.7 %all-gather.68.cloned.1.call-start = ((), (), s32[]{:S(2)}) async-start(), calls=%async_computation.24 | async-start | bytes 7077888 | tf_op jit(solution)/shard_map/all_gather | solution.py:443
  1402.2 186.8 %all-gather.66.cloned.1.call-start = ((), (), s32[]{:S(2)}) async-start(), calls=%async_computation.23 | async-start | bytes 7077888 | tf_op jit(solution)/shard_map/all_gather | solution.py:443
  1402.8 100.0 %all-to-all-start.4 = ((f32[8,96,16,96]{3,2,1,0:T(8,128)}), f32[8,96,16,96]{3,2,1,0:T(8,128)}, u32[]{:S(2)}, u32[]{:S(2)}) async-start(f32[8,96,16,96]{3,2,1,0:T(8,128)} %get-tuple-element.156), calls=%async_computation.4 | async-start | bytes 12582912 | tf_op jit(solution)/shard_map/all_to_all | solution.py:437
  1406.4 219.8 %all-gather.64.cloned.1.call-start = ((), (), s32[]{:S(2)}) async-start(), calls=%async_computation.22 | async-start | bytes 7077888 | tf_op jit(solution)/shard_map/all_gather | solution.py:443
  1621.2 89.6 %all-to-all-start.6 = ((f32[8,96,16,96]{3,2,1,0:T(8,128)}), f32[8,96,16,96]{3,2,1,0:T(8,128)}, u32[]{:S(2)}, u32[]{:S(2)}) async-start(f32[8,96,16,96]{3,2,1,0:T(8,128)} %get-tuple-element.166), calls=%async_computation.6 | async-start | bytes 12582912 | tf_op jit(solution)/shard_map/all_to_all | solution.py:437
  1710.8 75.0 %all-to-all-start.5 = ((f32[8,96,16,96]{3,2,1,0:T(8,128)}), f32[8,96,16,96]{3,2,1,0:T(8,128)}, u32[]{:S(2)}, u32[]{:S(2)}) async-start(f32[8,96,16,96]{3,2,1,0:T(8,128)} %bitcast.61), calls=%async_computation.5 | async-start | bytes 12582912 | tf_op jit(solution)/shard_map/all_to_all | solution.py:447
Sparse Core Ops, SparseCore 0:
  12.0 115.6 all-gather.37
  129.5 66.4 all-gather.35
  197.8 66.4 all-gather.33
  427.4 39.4 all-gather.43
  468.5 39.8 all-gather.41
  510.0 39.8 all-gather.39
  598.8 84.8 all-gather.49
  685.5 53.2 all-gather.47
  740.7 39.8 all-gather.45
  866.9 84.7 all-gather.55
  953.6 53.1 all-gather.53
  1008.5 39.8 all-gather.51
  1134.4 84.6 all-gather.61
  1220.9 53.2 all-gather.59
  1275.8 39.8 all-gather.57
  1402.4 84.7 all-gather.67
  1488.8 53.1 all-gather.65
  1543.7 39.8 all-gather.63
where the time goes:
time: 1810 us; the launch traced here: 1800 us
  Pallas kernels  1140 us (63%)
  waiting for transfers between devices  410 us (23%)
  local copies, waits for them, and re-layouts  159 us (9%)
  other arithmetic  47.3 us (3%)
  starting transfers between devices  26.5 us (1%)
    pallas_call x18, Pallas kernels, full_call(): pl.pallas_call(functools.partial(full_body, gathered=u_part.ndim == 4), g...  583 us
    all_to_all x6, waiting for transfers between devices, device_body(): lax.all_to_all(leaving, AXIS_NAME, split_axis=0, concat_axis=0, tiled=False)  402 us
    pallas_call x8, Pallas kernels, one_sided_call(): pl.pallas_call(functools.partial(one_sided_body, parts=parts, resume=resu...  303 us
    pallas_call x6, Pallas kernels, finish_call(): pl.pallas_call(functools.partial(finish_body, num=num, vec_size=vec_size)...  126 us
    pallas_call x1, Pallas kernels, exchange_call(): pl.pallas_call(functools.partial(exchange_body, num=num), in_specs=[vmem]...  87.3 us
    unnamed x10, local copies, waits for them, and re-layouts  45.2 us
    transpose x6, local copies, waits for them, and re-layouts, device_body(): leaving = nxt.transpose(2, 0, 1).reshape(num, slab, nq, slab)  39.7 us
  transfers between devices with their start and end apart: 25, of which 6 were waited for; matrix products, arithmetic and copies ran while one was open for 11% of the time, Pallas kernels for 48%

commit v1 on v0

--- a/solution.py
+++ b/solution.py
@@ -11,7 +11,7 @@
 LANCZOS_STEPS = 6
 AXIS_NAME = 'terms'
 GROUP = 4
-CHUNK = 256
+CHUNK = 384
 ROW_TILE = 16
 BF16 = jnp.bfloat16
 F32 = jnp.float32
@@ -46,13 +46,14 @@
     def _():
         pair = pair_ref[...].reshape(GROUP * nq * ROW_TILE, nq * ROW_TILE)
         for ci in range(parts):
-            for bt in range(nb // ROW_TILE):
-                rows = pl.ds(bt * ROW_TILE, ROW_TILE)
-                y = u_refs[ci][:, rows, :].reshape(nq * ROW_TILE, nc)
+            for bt in range(0, nb // ROW_TILE, 2):
+                rows = [pl.ds((bt + k) * ROW_TILE, ROW_TILE) for k in range(2)]
+                y = jnp.concatenate([u_refs[ci][:, rows[k], :].reshape(nq * ROW_TILE, nc) for k in range(2)], axis=1)
                 z = jnp.dot(pair, y, preferred_element_type=F32).astype(BF16)
-                z = z.reshape(GROUP, nq, ROW_TILE, nc)
-                for t in range(GROUP):
-                    z_ref[:, rows, (ci * GROUP + t) * nc:(ci * GROUP + t + 1) * nc] = z[t]
+                for k in range(2):
+                    part = z[:, k * nc:(k + 1) * nc].reshape(GROUP, nq, ROW_TILE, nc)
+                    for t in range(GROUP):
+                        z_ref[:, rows[k], (ci * GROUP + t) * nc:(ci * GROUP + t + 1) * nc] = part[t]
 
     for h in range(2):
         @pl.when(grp < split_ref[0])
@@ -72,7 +73,7 @@
             pltpu.make_async_copy(sigma_ref.at[pl.ds(h * half, half)], sigma_out.at[pl.ds(h * half, half)], out_sem.at[h]).wait()
 
 
-def full_body(order_ref, split_ref, u_hbm, right_ref, pair_ref, *rest, gathered):
+def full_body(order_ref, split_ref, u_hbm, right_ref, pair_ref, *rest, gathered, chunk):
     left_refs = rest[:GROUP]
     sigma_in, _, sigma_out, _, sigma_ref, u_ref, y_ref, z_ref, u_sem, in_sem, out_sem = rest[GROUP:]
     grp = pl.program_id(0)
@@ -83,9 +84,10 @@
     half = nq // 2
 
     def u_copy(r):
+        cols = pl.ds(chunk * nc, nc)
         if gathered:
-            return pltpu.make_async_copy(u_hbm.at[:, r], u_ref.at[:, r], u_sem.at[r])
-        return pltpu.make_async_copy(u_hbm.at[r], u_ref.at[r], u_sem.at[r])
+            return pltpu.make_async_copy(u_hbm.at[:, r, :, cols], u_ref.at[:, r], u_sem.at[r])
+        return pltpu.make_async_copy(u_hbm.at[r, :, cols], u_ref.at[r], u_sem.at[r])
 
     @pl.when((grp == 0) & (split_ref[0] < num_grp))
     def _():
@@ -93,22 +95,39 @@
             u_copy(r).start()
         pltpu.make_async_copy(sigma_in, sigma_ref, in_sem).start()
 
+    def stage_right(first, last):
+        right = right_ref[...].reshape(GROUP * nb, nd)
+        for r in range(first, last, 2):
+            u = jnp.concatenate([(u_ref[:, r + k] if gathered else u_ref[r + k]).reshape(nd, nc) for k in range(2)], axis=1)
+            y = jnp.dot(right, u, preferred_element_type=F32).astype(BF16)
+            for k in range(2):
+                y_ref[r + k] = y[:, k * nc:(k + 1) * nc]
+
+    head = nq // 4
+
     @pl.when(grp == split_ref[0])
     def _():
-        for r in range(nq):
+        for r in range(head):
             u_copy(r).wait()
 
     @pl.when(grp >= split_ref[0])
     def _():
-        right = right_ref[...].reshape(GROUP * nb, nd)
-        for r in range(nq):
-            u = (u_ref[:, r] if gathered else u_ref[r]).reshape(nd, nc)
-            y_ref[r] = jnp.dot(right, u, preferred_element_type=F32).astype(BF16)
+        stage_right(0, head)
+
+    @pl.when(grp == split_ref[0])
+    def _():
+        for r in range(head, nq):
+            u_copy(r).wait()
+
+    @pl.when(grp >= split_ref[0])
+    def _():
+        stage_right(head, nq)
         for t in range(GROUP):
-            for bt in range(nb // ROW_TILE):
-                y = y_ref[:, pl.ds(t * nb + bt * ROW_TILE, ROW_TILE), :].reshape(nq * ROW_TILE, nc)
+            for bt in range(0, nb // ROW_TILE, 2):
+                y = jnp.concatenate([y_ref[:, pl.ds(t * nb + (bt + k) * ROW_TILE, ROW_TILE), :].reshape(nq * ROW_TILE, nc) for k in range(2)], axis=1)
                 z = jnp.dot(pair_ref[t], y, preferred_element_type=F32).astype(BF16)
-                z_ref[:, pl.ds(bt * ROW_TILE, ROW_TILE), t * nc:(t + 1) * nc] = z.reshape(nq, ROW_TILE, nc)
+                for k in range(2):
+                    z_ref[:, pl.ds((bt + k) * ROW_TILE, ROW_TILE), t * nc:(t + 1) * nc] = z[:, k * nc:(k + 1) * nc].reshape(nq, ROW_TILE, nc)
 
     @pl.when(grp == split_ref[0])
     def _():
@@ -136,13 +155,10 @@
 VMEM_LIMIT = 63 << 20
 
 
-def whole(shape):
-    return pl.BlockSpec(shape, lambda g, o, s: (0,) * len(shape), pipeline_mode=pl.Buffered(1))
-
-
 def one_sided_call(order, split, u_parts, pair_blk, left_parts, carried, sigma=None):
     parts = len(u_parts)
-    nq, nb, nc = u_parts[0].shape
+    nq, nb, _ = u_parts[0][0].shape
+    nc = CHUNK
     na = left_parts[0].shape[2]
     terms = pair_blk.shape[0]
     nk = nq * ROW_TILE
@@ -160,7 +176,8 @@
         functools.partial(one_sided_body, parts=parts, resume=resume),
         grid_spec=pltpu.PrefetchScalarGridSpec(
             num_scalar_prefetch=2, grid=(terms // GROUP,),
-            in_specs=[whole((nq, nb, nc))] * parts + [pl.BlockSpec((GROUP, nk, nk), lambda g, o, s: (clamp(g, s), 0, 0))] + left_specs
+            in_specs=[pl.BlockSpec((nq, nb, nc), functools.partial(lambda g, o, s, c: (0, 0, c), c=c), pipeline_mode=pl.Buffered(1)) for _, c in u_parts]
+            + [pl.BlockSpec((GROUP, nk, nk), lambda g, o, s: (clamp(g, s), 0, 0))] + left_specs
             + [ANY] * (2 if resume else 1),
             out_specs=[ANY, ANY],
             scratch_shapes=[pltpu.VMEM((nq, nb, na), F32), pltpu.VMEM((nq, nb, parts * GROUP * nc), BF16),
@@ -170,12 +187,12 @@
         compiler_params=pltpu.CompilerParams(dimension_semantics=('arbitrary',), vmem_limit_bytes=VMEM_LIMIT),
         cost_estimate=pl.CostEstimate(flops=n * 2 * nq * nb * parts * nc * (na + nk), bytes_accessed=n * na * nc * parts * 2, transcendentals=0),
         name='one_sided',
-    )(order, split, *u_parts, pair_blk, *[left_parts[c] for c in range(parts) for _ in range(GROUP)], *([sigma] if resume else []), carried)
-
-
-def full_call(order, split, u_part, right_slab, pair_blk, left_part, sigma, carried):
+    )(order, split, *[u for u, _ in u_parts], pair_blk, *[left_parts[c] for c in range(parts) for _ in range(GROUP)], *([sigma] if resume else []), carried)
+
+
+def full_call(order, split, u_part, chunk, right_slab, pair_blk, left_part, sigma, carried):
     nq, nb, na = sigma.shape
-    nc = u_part.shape[-1]
+    nc = CHUNK
     terms, _, nd = right_slab.shape
     nk = nq * ROW_TILE
 
@@ -186,38 +203,40 @@
                   for t in range(GROUP)]
     n = terms // 2
     return pl.pallas_call(
-        functools.partial(full_body, gathered=u_part.ndim == 4),
+        functools.partial(full_body, gathered=u_part.ndim == 4, chunk=chunk),
         grid_spec=pltpu.PrefetchScalarGridSpec(
             num_scalar_prefetch=2, grid=(terms // GROUP,),
             in_specs=[ANY,
                       pl.BlockSpec((GROUP, nb, nd), lambda g, o, s: (at_least(g, s), 0, 0)),
                       pl.BlockSpec((GROUP, nk, nk), lambda g, o, s: (at_least(g, s), 0, 0))] + left_specs + [ANY, ANY],
             out_specs=[ANY, ANY],
-            scratch_shapes=[pltpu.VMEM((nq, nb, na), F32), pltpu.VMEM(u_part.shape, BF16),
+            scratch_shapes=[pltpu.VMEM((nq, nb, na), F32), pltpu.VMEM(u_part.shape[:-1] + (nc,), BF16),
                             pltpu.VMEM((nq, GROUP * nb, nc), BF16), pltpu.VMEM((nq, nb, GROUP * nc), BF16),
                             pltpu.SemaphoreType.DMA((nq,)), pltpu.SemaphoreType.DMA, pltpu.SemaphoreType.DMA((2,))]),
         out_shape=[jax.ShapeDtypeStruct((nq, nb, na), F32), jax.ShapeDtypeStruct(carried.shape, carried.dtype)],
         input_output_aliases={2 + 3 + GROUP: 0, 2 + 4 + GROUP: 1},
         compiler_params=pltpu.CompilerParams(dimension_semantics=('arbitrary',), vmem_limit_bytes=VMEM_LIMIT),
-        cost_estimate=pl.CostEstimate(flops=n * 2 * nq * nb * nc * (nd + na + nk), bytes_accessed=n * na * nc * 2 + u_part.size * 2, transcendentals=0),
+        cost_estimate=pl.CostEstimate(flops=n * 2 * nq * nb * nc * (nd + na + nk), bytes_accessed=n * na * nc * 2 + nq * nd * nc * 2, transcendentals=0),
         name='full_terms',
     )(order, split, u_part, right_slab, pair_blk, *[left_part] * GROUP, sigma, carried)
 
 
-def place_body(*refs, num, width):
+def place_body(*refs, num, nq, width):
     x_ref, out_ref = refs[0], refs[-1]
-    for src in range(num):
-        out_ref[0, :, :, src * width:(src + 1) * width] = x_ref[src]
+    for q0 in range(0, nq, 8):
+        lines = [jnp.concatenate([x_ref[src, :, q * width:(q + 1) * width] for src in range(num)], axis=1) for q in range(q0, q0 + 8)]
+        out_ref[0, :, q0:q0 + 8, :] = jnp.swapaxes(jnp.stack(lines, axis=0), 0, 1)
 
 
 def place_call(arrived, krylov, index):
-    num, rows, nq, width = arrived.shape
+    num, rows, size = arrived.shape
+    nq, wide = krylov.shape[2:]
     blk = rows // 4
     return pl.pallas_call(
-        functools.partial(place_body, num=num, width=width),
+        functools.partial(place_body, num=num, nq=nq, width=wide // num),
         grid=(4,),
-        in_specs=[pl.BlockSpec((num, blk, nq, width), lambda i: (0, i, 0, 0)), ANY],
-        out_specs=pl.BlockSpec((1, blk, nq, num * width), lambda i: (index, i, 0, 0)),
+        in_specs=[pl.BlockSpec((num, blk, size), lambda i: (0, i, 0)), ANY],
+        out_specs=pl.BlockSpec((1, blk, nq, wide), lambda i: (index, i, 0, 0)),
         out_shape=jax.ShapeDtypeStruct(krylov.shape, krylov.dtype),
         input_output_aliases={1: 0},
         compiler_params=pltpu.CompilerParams(dimension_semantics=('arbitrary',), vmem_limit_bytes=VMEM_LIMIT),
@@ -246,32 +265,85 @@
     )(me, norm_tile, wavefunction)
 
 
-def exchange_body(x_ref, out_ref, send_sem, recv_sem, *, num):
+def exchange_body(x_ref, psi_hbm, out_ref, norm_ref, stage_ref, psi_ref, psi_sem, send_sem, recv_sem, *, num, vec_size):
     me = lax.axis_index(AXIS_NAME)
+    rows = psi_ref.shape[0]
+    blk = rows // FIN_BLOCKS
+    small = x_ref.shape[0]
+
+    def load(i):
+        return pltpu.make_async_copy(psi_hbm.at[pl.ds(me * rows + i * blk, blk)], psi_ref.at[pl.ds(i * blk, blk)], psi_sem.at[i])
+
+    for i in range(FIN_BLOCKS):
+        load(i).start()
     barrier = pltpu.get_barrier_semaphore()
     for off in range(1, num):
         pl.semaphore_signal(barrier, inc=1, device_id=(lax.rem(me + off, num),), device_id_type=pl.DeviceIdType.MESH)
+    stage_ref[:small] = x_ref[...]
+    part = jnp.zeros((8, 128), F32)
+    for i in range(FIN_BLOCKS):
+        load(i).wait()
+        part = lax.fori_loop(i * blk, (i + 1) * blk, lambda a, acc: acc + fold(psi_ref[a] * psi_ref[a]), part)
+    stage_ref[small:] = part
     pl.semaphore_wait(barrier, num - 1)
     copies = []
     for off in range(1, num):
         copies.append(pltpu.make_async_remote_copy(
-            src_ref=x_ref, dst_ref=out_ref.at[me], send_sem=send_sem.at[off - 1], recv_sem=recv_sem.at[off - 1],
+            src_ref=stage_ref, dst_ref=out_ref.at[me], send_sem=send_sem.at[off - 1], recv_sem=recv_sem.at[off - 1],
             device_id=(lax.rem(me + off, num),), device_id_type=pl.DeviceIdType.MESH))
     for copy in copies:
         copy.start()
-    out_ref[me] = x_ref[...]
+    out_ref[me] = stage_ref[...]
     for copy in copies:
         copy.wait()
-
-
-def exchange_call(x, num):
+    total = out_ref[0, small:]
+    for src in range(1, num):
+        total = total + out_ref[src, small:]
+    norm_ref[...] = jnp.sqrt(jnp.full((8, 128), jnp.sum(total) / vec_size, F32))
+
+
+def exchange_call(x, wavefunction, num):
     vmem = pl.BlockSpec(memory_space=pltpu.VMEM)
-    return pl.pallas_call(
-        functools.partial(exchange_body, num=num), in_specs=[vmem], out_specs=vmem,
-        out_shape=jax.ShapeDtypeStruct((num,) + x.shape, x.dtype),
-        scratch_shapes=[pltpu.SemaphoreType.DMA((num - 1,))] * 2,
+    bond, nq, width = wavefunction.shape
+    size = x.shape[0] + 8
+    return pl.pallas_call(
+        functools.partial(exchange_body, num=num, vec_size=wavefunction.size), in_specs=[vmem, ANY], out_specs=[vmem, vmem],
+        out_shape=[jax.ShapeDtypeStruct((num, size, 128), F32), jax.ShapeDtypeStruct((8, 128), F32)],
+        scratch_shapes=[pltpu.VMEM((size, 128), F32), pltpu.VMEM((bond // num, nq, width), F32), pltpu.SemaphoreType.DMA((FIN_BLOCKS,))]
+        + [pltpu.SemaphoreType.DMA((num - 1,))] * 2,
         compiler_params=pltpu.CompilerParams(collective_id=20, has_side_effects=True, vmem_limit_bytes=VMEM_LIMIT),
-        name='exchange')(x)
+        name='exchange')(x, wavefunction)
+
+
+def spread_body(me_ref, norm_ref, psi_ref, wide_ref, cur_ref, low_ref, turn_ref):
+    nq, nb, _ = cur_ref.shape
+    rows = pl.ds(pl.multiple_of(me_ref[0] * nb, 8), nb)
+    norm = norm_ref[:1, :1]
+    for q in range(nq):
+        turn_ref[q % 2] = (psi_ref[:, q, :] / norm).T
+        wide_ref[q] = turn_ref[q % 2].astype(BF16)
+        own = turn_ref[q % 2, rows, :]
+        cur_ref[q] = own
+        low_ref[q] = own.astype(BF16)
+
+
+def spread_call(wavefunction, norm_tile, me, slab):
+    bond, nq, width = wavefunction.shape
+    blk = 128
+    return pl.pallas_call(
+        spread_body,
+        grid_spec=pltpu.PrefetchScalarGridSpec(
+            num_scalar_prefetch=1, grid=(bond // blk,),
+            in_specs=[pl.BlockSpec((8, 128), lambda i, m: (0, 0)), pl.BlockSpec((blk, nq, width), lambda i, m: (i, 0, 0))],
+            out_specs=[pl.BlockSpec((nq, width, blk), lambda i, m: (0, 0, i)), pl.BlockSpec((nq, slab, blk), lambda i, m: (0, 0, i)),
+                       pl.BlockSpec((nq, slab, blk), lambda i, m: (0, 0, i))],
+            scratch_shapes=[pltpu.VMEM((2, width, blk), F32)]),
+        out_shape=[jax.ShapeDtypeStruct((nq, width, bond), BF16), jax.ShapeDtypeStruct((nq, slab, bond), F32),
+                   jax.ShapeDtypeStruct((nq, slab, bond), BF16)],
+        compiler_params=pltpu.CompilerParams(dimension_semantics=('arbitrary',), vmem_limit_bytes=VMEM_LIMIT),
+        cost_estimate=pl.CostEstimate(flops=wavefunction.size, bytes_accessed=8 * wavefunction.size, transcendentals=0),
+        name='spread',
+    )(me, norm_tile, wavefunction)
 
 
 def sum_over_devices(slot_ref, value, send_sem, recv_sem, me, num):
@@ -301,7 +373,7 @@
     return out
 
 
-def finish_body(beta_prev_ref, sigma_hbm, cur_hbm, prev_hbm, next_hbm, u0, u1, u2, alpha_ref, beta_ref,
+def finish_body(beta_prev_ref, sigma_hbm, cur_hbm, prev_hbm, next_hbm, u0, u1, alpha_ref, beta_ref,
                 sigma_ref, cur_ref, prev_ref, low_ref, slot_a, slot_b, in_sem, out_sem, send_a, recv_a, send_b, recv_b, *, num, vec_size):
     me = lax.axis_index(AXIS_NAME)
     nq, _, _ = sigma_ref.shape
@@ -354,7 +426,7 @@
         rows = pl.ds(i * blk, blk)
         return [pltpu.make_async_copy(cur_ref.at[rows], next_hbm.at[rows], out_sem.at[0, i])] + [
             pltpu.make_async_copy(low_ref.at[rows, :, pl.ds(n * CHUNK, CHUNK)], ref.at[rows], out_sem.at[1 + n, i])
-            for n, ref in enumerate((u0, u1, u2))]
+            for n, ref in enumerate((u0, u1))]
 
     for i in range(FIN_BLOCKS):
         lax.fori_loop(i * blk, (i + 1) * blk, scale_part, 0)
@@ -371,11 +443,11 @@
     return pl.pallas_call(
         functools.partial(finish_body, num=num, vec_size=vec_size),
         in_specs=[pl.BlockSpec(memory_space=pltpu.SMEM)] + [ANY] * 3,
-        out_specs=[ANY] * 4 + [vmem] * 2,
-        out_shape=[jax.ShapeDtypeStruct((nq, nb, na), F32)] + [jax.ShapeDtypeStruct((nq, nb, CHUNK), BF16)] * 3
+        out_specs=[ANY] * 3 + [vmem] * 2,
+        out_shape=[jax.ShapeDtypeStruct((nq, nb, na), F32)] + [jax.ShapeDtypeStruct((nq, nb, CHUNK), BF16)] * 2
         + [jax.ShapeDtypeStruct((8, 128), F32)] * 2,
         scratch_shapes=[pltpu.VMEM((nq, nb, na), F32)] * 3 + [pltpu.VMEM((nq, nb, na), BF16)] + [pltpu.VMEM((num, 8, 128), F32)] * 2
-        + [pltpu.SemaphoreType.DMA((3, FIN_BLOCKS)), pltpu.SemaphoreType.DMA((4, FIN_BLOCKS))] + [pltpu.SemaphoreType.DMA((num - 1,))] * 4,
+        + [pltpu.SemaphoreType.DMA((3, FIN_BLOCKS)), pltpu.SemaphoreType.DMA((3, FIN_BLOCKS))] + [pltpu.SemaphoreType.DMA((num - 1,))] * 4,
         compiler_params=pltpu.CompilerParams(collective_id=call_id, has_side_effects=True, vmem_limit_bytes=VMEM_LIMIT),
         cost_estimate=pl.CostEstimate(flops=10 * sigma.size, bytes_accessed=22 * sigma.size, transcendentals=0),
         name='finish',
@@ -394,7 +466,7 @@
 
         terms_loc = pair_loc.shape[0]
         small = jnp.concatenate([pair_loc.astype(F32).reshape(8, 128), jnp.pad(flag_loc.astype(F32), (0, 1024 - terms_loc)).reshape(8, 128)])
-        small_all = exchange_call(small, num)
+        small_all, norm_tile = exchange_call(small, wavefunction, num)
         right_slab = lax.all_to_all(right_loc, AXIS_NAME, split_axis=1, concat_axis=0, tiled=True)
         left_parts = []
         for i in range(nchunk):
@@ -409,13 +481,11 @@
         pair_sorted = pair_all[order]
         pair_blk = (pair_sorted[:, :, None, :, None] * eye[None, None, :, None, :]).reshape(-1, nq * ROW_TILE, nq * ROW_TILE)
 
-        norm0 = jnp.sqrt(jnp.sum(wavefunction * wavefunction) / vec_size)
-        krylov = first_call(wavefunction, jnp.full((8, 128), norm0, F32), me.reshape(1).astype(jnp.int32), slab, LANCZOS_STEPS + 1)
-        cur = (lax.dynamic_slice_in_dim(wavefunction, me * slab, slab, axis=2) / norm0).transpose(1, 2, 0)
-        cur_low = cur.astype(BF16)
-        u_parts = [cur_low[:, :, i * CHUNK:(i + 1) * CHUNK] for i in range(nchunk)]
-        whole_low = (wavefunction / norm0).astype(BF16).transpose(1, 2, 0)
-        u_wide = [whole_low[:, :, i * CHUNK:(i + 1) * CHUNK] for i in range(nchunk)]
+        here = me.reshape(1).astype(jnp.int32)
+        krylov = first_call(wavefunction, norm_tile, here, slab, LANCZOS_STEPS + 1)
+        u_wide, cur, cur_low = spread_call(wavefunction, norm_tile, here, slab)
+        u_parts = [(cur_low, i) for i in range(nchunk)]
+        u_wide = [(u_wide, i) for i in range(nchunk)]
         prev = jnp.zeros_like(cur)
         beta_prev = jnp.zeros((1,), F32)
         tiles = []
@@ -425,24 +495,24 @@
                 sigma = None
                 for i in range(nchunk):
                     sigma, krylov = one_sided_call(order, split, u_parts[i:i + 1], pair_blk, left_parts[i:i + 1], krylov, sigma)
-                    sigma, krylov = full_call(order, split, u_wide[i], right_slab, pair_blk, left_parts[i], sigma, krylov)
+                    sigma, krylov = full_call(order, split, *u_wide[i], right_slab, pair_blk, left_parts[i], sigma, krylov)
             else:
                 if arriving is None:
                     sigma, krylov = one_sided_call(order, split, u_parts, pair_blk, left_parts, krylov)
                 else:
                     sigma, arriving = one_sided_call(order, split, u_parts, pair_blk, left_parts, arriving)
                     krylov = place_call(arriving, krylov, step - 1)
-                sigma, krylov = full_call(order, split, u_wide[0], right_slab, pair_blk, left_parts[0], sigma, krylov)
-                sigma, leaving = full_call(order, split, u_wide[1], right_slab, pair_blk, left_parts[1], sigma, leaving)
+                sigma, leaving = full_call(order, split, *u_wide[0], right_slab, pair_blk, left_parts[0], sigma, leaving)
                 arriving = lax.all_to_all(leaving, AXIS_NAME, split_axis=0, concat_axis=0, tiled=False)
-                sigma, krylov = full_call(order, split, u_wide[2], right_slab, pair_blk, left_parts[2], sigma, krylov)
-            nxt, *u_parts, alpha_t, beta_t = finish_call(beta_prev, sigma, cur, prev, num, vec_size, step)
+                sigma, krylov = full_call(order, split, *u_wide[1], right_slab, pair_blk, left_parts[1], sigma, krylov)
+            nxt, *lows, alpha_t, beta_t = finish_call(beta_prev, sigma, cur, prev, num, vec_size, step)
             beta_prev = beta_t[0, :1]
             tiles += [alpha_t[0, :1], beta_prev]
             if step + 1 < LANCZOS_STEPS:
-                u_wide = [lax.all_gather(part, AXIS_NAME, axis=0, tiled=False) for part in u_parts]
+                u_parts = [(low, 0) for low in lows]
+                u_wide = [(lax.all_gather(low, AXIS_NAME, axis=0, tiled=False), 0) for low in lows]
             prev, cur = cur, nxt
-            leaving = nxt.transpose(2, 0, 1).reshape(num, slab, nq, slab)
+            leaving = nxt.reshape(nq * slab, bond).T.reshape(num, slab, nq * slab)
         krylov = place_call(arriving, krylov, LANCZOS_STEPS - 1)
         arriving = lax.all_to_all(leaving, AXIS_NAME, split_axis=0, concat_axis=0, tiled=False)
         krylov = place_call(arriving, krylov, LANCZOS_STEPS)

time: 1810 us -> 1560 us (0.86)
  waiting for transfers between devices: 410 us -> 313 us
  Pallas kernels: 1140 us -> 1070 us
  local copies, waits for them, and re-layouts: 159 us -> 112 us
  other arithmetic: 47.3 us -> 11.7 us
    all_to_all x6, waiting for transfers between devices: 402 us -> 302 us  [device_body(): lax.all_to_all(leaving, AXIS_NAME, split_axis=0, concat_axis=0, tiled=False)]
    transpose x6 -> x0, local copies, waits for them, and re-layouts: 39.7 us -> none  [device_body(): leaving = nxt.transpose(2, 0, 1).reshape(num, slab, nq, slab)]
    reshape x0 -> x6, local copies, waits for them, and re-layouts: none -> 38.6 us  [device_body(): leaving = nxt.reshape(nq * slab, bond).T.reshape(num, slab, nq * slab)]
    unnamed x10 -> x7, local copies, waits for them, and re-layouts: 45.2 us -> 8.52 us
    pallas_call x6, Pallas kernels: 126 us -> 96.4 us  [finish_call(): pl.pallas_call(functools.partial(finish_body, num=num, vec_size=vec_size)...]
    pallas_call x25 -> x20, Pallas kernels: 706 us -> 677 us  [the longest x12 536 us: full_call(): pl.pallas_call(functools.partial(full_body, gathered=u_part.ndim == 4, ch...]
    pallas_call x8 -> x7, Pallas kernels: 303 us -> 293 us  [one_sided_call(): pl.pallas_call(functools.partial(one_sided_body, parts=parts, resume=resu...]
  transfers between devices with their start and end apart: 25 -> 19, of which waited for: 6 -> 6; matrix products, arithmetic and copies ran while one was open for 11% -> 8% of each run, Pallas kernels for 48% -> 47%
where the time goes in v1:
time: 1560 us; the launch traced here: 1550 us
  Pallas kernels  1070 us (69%)
  waiting for transfers between devices  313 us (20%)
  local copies, waits for them, and re-layouts  112 us (7%)
  starting transfers between devices  25.1 us (2%)
    pallas_call x12, Pallas kernels, full_call(): pl.pallas_call(functools.partial(full_body, gathered=u_part.ndim == 4, ch...  536 us
    all_to_all x6, waiting for transfers between devices, device_body(): lax.all_to_all(leaving, AXIS_NAME, split_axis=0, concat_axis=0, tiled=False)  302 us
    pallas_call x7, Pallas kernels, one_sided_call(): pl.pallas_call(functools.partial(one_sided_body, parts=parts, resume=resu...  293 us
    pallas_call x6, Pallas kernels, finish_call(): pl.pallas_call(functools.partial(finish_body, num=num, vec_size=vec_size)...  96.4 us
    pallas_call x1, Pallas kernels, exchange_call(): pl.pallas_call(functools.partial(exchange_body, num=num, vec_size=wavefun...  76.2 us
    reshape x6, local copies, waits for them, and re-layouts, device_body(): leaving = nxt.reshape(nq * slab, bond).T.reshape(num, slab, nq * slab)  38.6 us
    pallas_call x6, Pallas kernels, place_call(): pl.pallas_call(functools.partial(place_body, num=num, nq=nq, width=wide /...  37.4 us
  transfers between devices with their start and end apart: 19, of which 6 were waited for; matrix products, arithmetic and copies ran while one was open for 8% of the time, Pallas kernels for 47%

profile of v1, /device:TPU:0, one launch (start us, length us, event | category | flops | bytes accessed | tf_op | source)
XLA Modules:
  0.0 1549.0 jit_solution(5408141133307097464)
XLA Ops:
  7.2 4.8 fusion.2
  12.8 8.5 copy.69
  21.3 4.0 all-to-all-start
  26.2 76.2 %exchange.1 = (f32[8,24,128]{2,1,0:T(8,128)}, f32[8,128]{1,0:T(8,128)}) custom-call(f32[16,128]{1,0:T(8,128)} %pad_maximum_fusion.x_ref, f32[768,16,768]{2,1,0:T(8,128)} %psi_ref.3), custom_call_target="tpu_custom_call" | custom-call | tf_op jit(solution)/shard_map/exchange/pallas_call | solution.py:309
  105.4 1.6 sort.17
  107.8 6.4 mul.24
  114.2 16.2 %copy.73 = bf16[32,256,256]{2,1,0:T(8,128)(2,1)} copy(bf16[32,256,256]{0,2,1:T(8,128)(2,1)} %bitcast.58) | data formatting | bytes 8388608 | tf_op jit(solution)/shard_map/mul | solution.py:482
  131.6 5.1 first.1.rest_6_
  136.7 27.5 %spread.1 = (bf16[16,768,768]{2,1,0:T(8,128)(2,1)}, f32[16,96,768]{2,1,0:T(8,128)}, bf16[16,96,768]{2,1,0:T(8,128)(2,1)}) custom-call(s32[1]{0:T(128)} %bitcast.2.me_ref, f32[8,128]{1,0:T(8,128)} %get-tuple-element.77.norm_ref, f32[768,16,768]{2,1,0:T(8,128)} %psi_ref.3), custom_call_target="tpu_custom_call" | custom-call | flops 9437184 | bytes 75497472 | tf_op jit(solution)/shard_map/spread/pallas_call | solution.py:333
  164.4 5.2 broadcast_multiply_fusion.rest_1_.pair_ref.rest_2_
  169.6 2.9 copy.70
  172.9 2.8 bitcast_select_fusion
  175.7 5.3 gather_fusion
  181.0 27.0 %one_sided.7 = (f32[16,96,768]{2,1,0:T(8,128)}, f32[7,96,16,768]{3,2,1,0:T(8,128)}) custom-call(s32[32]{0:T(128)} %copy-done, s32[1]{0:T(128)} %bitcast.1.split_ref, bf16[16,96,768]{2,1,0:T(8,128)(2,1)} %get-tuple-element.79.rest_0_, bf16[32,256,256]{2,1,0:T(8,128)(2,1)} %broadcast_multiply_fusion.rest_1_.pair_ref.rest_2_, ...), custom_call_target="tpu_custom_call", output_to_operand_aliasing={{1}: (8, {})} | custom-call | flops 19327352832 | bytes 9437184 | tf_op jit(solution)/shard_map/one_sided/pallas_call | solution.py:175
  207.9 44.4 %full_terms.12 = (f32[16,96,768]{2,1,0:T(8,128)}, f32[7,96,16,768]{3,2,1,0:T(8,128)}) custom-call(s32[32]{0:T(128)} %copy-done, s32[1]{0:T(128)} %bitcast.1.split_ref, bf16[16,768,768]{2,1,0:T(8,128)(2,1)} %get-tuple-element.78.u_hbm, bf16[32,96,768]{2,1,0:T(8,128)(2,1)} %gather_fusion, ...), custom_call_target="tpu_custom_call", output_to_operand_aliasing={{0}: (9, {}), {1}: (10, {})} | custom-call | flops 33822867456 | bytes 18874368 | tf_op jit(solution)/shard_map/full_terms/pallas_call | solution.py:205
  252.4 29.3 %one_sided.8 = (f32[16,96,768]{2,1,0:T(8,128)}, f32[7,96,16,768]{3,2,1,0:T(8,128)}) custom-call(s32[32]{0:T(128)} %copy-done, s32[1]{0:T(128)} %bitcast.1.split_ref, bf16[16,96,768]{2,1,0:T(8,128)(2,1)} %get-tuple-element.79.rest_0_, ...), custom_call_target="tpu_custom_call", output_to_operand_aliasing={{0}: (8, {}), {1}: (9, {})} | custom-call | flops 19327352832 | bytes 9437184 | tf_op jit(solution)/shard_map/one_sided/pallas_call | solution.py:175
  281.7 44.5 %full_terms.13 = (f32[16,96,768]{2,1,0:T(8,128)}, f32[7,96,16,768]{3,2,1,0:T(8,128)}) custom-call(s32[32]{0:T(128)} %copy-done, s32[1]{0:T(128)} %bitcast.1.split_ref, bf16[16,768,768]{2,1,0:T(8,128)(2,1)} %get-tuple-element.78.u_hbm, bf16[32,96,768]{2,1,0:T(8,128)(2,1)} %gather_fusion, ...), custom_call_target="tpu_custom_call", output_to_operand_aliasing={{0}: (9, {}), {1}: (10, {})} | custom-call | flops 33822867456 | bytes 18874368 | tf_op jit(solution)/shard_map/full_terms/pallas_call | solution.py:205
  326.3 2.6 broadcast_in_dim.32.prev_hbm
  328.9 15.6 %finish.6 = (f32[16,96,768]{2,1,0:T(8,128)}, bf16[16,96,384]{2,1,0:T(8,128)(2,1)}, bf16[16,96,384]{2,1,0:T(8,128)(2,1)}, f32[8,128]{1,0:T(8,128)}, f32[8,128]{1,0:T(8,128)}) custom-call(f32[1]{0:T(128)} %constant.10.clone.1.beta_prev_ref, f32[16,96,768]{2,1,0:T(8,128)} %get-tuple-element.86.sigma_hbm, f32[16,96,768]{2,1,0:T(8,128)} %get-tuple-element.87.cur_hbm.prev_hbm, ...), custom_call_target="tpu_custom_call" | custom-call | flops 11796480 | bytes 25952256 | tf_op jit(solution)/shard_map/finish/pallas_call | solution.py:443
  345.1 6.3 copy.74
  352.8 47.4 %one_sided.9 = (f32[16,96,768]{2,1,0:T(8,128)}, f32[7,96,16,768]{3,2,1,0:T(8,128)}) custom-call(s32[32]{0:T(128)} %copy-done, s32[1]{0:T(128)} %bitcast.1.split_ref, bf16[16,96,384]{2,1,0:T(8,128)(2,1)} %get-tuple-element.90.rest_0_, bf16[16,96,384]{2,1,0:T(8,128)(2,1)} %get-tuple-element.89.rest_1_, ...), custom_call_target="tpu_custom_call", output_to_operand_aliasing={{1}: (13, {})} | custom-call | flops 38654705664 | bytes 18874368 | tf_op jit(solution)/shard_map/one_sided/pallas_call | solution.py:175
  400.2 45.6 %full_terms.14 = (f32[16,96,768]{2,1,0:T(8,128)}, f32[8,96,1536]{2,1,0:T(8,128)}) custom-call(s32[32]{0:T(128)} %copy-done, s32[1]{0:T(128)} %bitcast.1.split_ref, bf16[8,16,96,384]{3,2,1,0:T(8,128)(2,1)} %bitcast.81, bf16[32,96,768]{2,1,0:T(8,128)(2,1)} %gather_fusion, ...), custom_call_target="tpu_custom_call", output_to_operand_aliasing={{0}: (9, {}), {1}: (10, {})} | custom-call | flops 33822867456 | bytes 18874368 | tf_op jit(solution)/shard_map/full_terms/pallas_call | solution.py:205
  445.7 6.9 all-gather.27.cloned.1.call-done
  452.7 44.6 %full_terms.15 = (f32[16,96,768]{2,1,0:T(8,128)}, f32[7,96,16,768]{3,2,1,0:T(8,128)}) custom-call(s32[32]{0:T(128)} %copy-done, s32[1]{0:T(128)} %bitcast.1.split_ref, bf16[8,16,96,384]{3,2,1,0:T(8,128)(2,1)} %bitcast.75, bf16[32,96,768]{2,1,0:T(8,128)(2,1)} %gather_fusion, ...), custom_call_target="tpu_custom_call", output_to_operand_aliasing={{0}: (9, {}), {1}: (10, {})} | custom-call | flops 33822867456 | bytes 18874368 | tf_op jit(solution)/shard_map/full_terms/pallas_call | solution.py:205
  497.3 16.1 %finish.7 = (f32[16,96,768]{2,1,0:T(8,128)}, bf16[16,96,384]{2,1,0:T(8,128)(2,1)}, bf16[16,96,384]{2,1,0:T(8,128)(2,1)}, f32[8,128]{1,0:T(8,128)}, f32[8,128]{1,0:T(8,128)}) custom-call(f32[1]{0:T(128)} %bitcast.7.beta_prev_ref, f32[16,96,768]{2,1,0:T(8,128)} %get-tuple-element.96.sigma_hbm, f32[16,96,768]{2,1,0:T(8,128)} %get-tuple-element.93.cur_hbm.prev_hbm, ...), custom_call_target="tpu_custom_call" | custom-call | flops 11796480 | bytes 25952256 | tf_op jit(solution)/shard_map/finish/pallas_call | solution.py:443
  514.1 3.3 all-to-all-start.1
  517.5 6.9 copy.75
  525.5 67.4 %all-to-all-done.1.rest_11_ = f32[8,96,1536]{2,1,0:T(8,128)} async-done(((f32[8,96,1536]{2,1,0:T(8,128)}), f32[8,96,1536]{2,1,0:T(8,128)}, u32[]{:S(2)}, u32[]{:S(2)}) %all-to-all-start.1) | async-done | bytes 4718624 | tf_op jit(solution)/shard_map/all_to_all | solution.py:506
  592.9 47.3 %one_sided.10 = (f32[16,96,768]{2,1,0:T(8,128)}, f32[8,96,1536]{2,1,0:T(8,128)}) custom-call(s32[32]{0:T(128)} %copy-done, s32[1]{0:T(128)} %bitcast.1.split_ref, bf16[16,96,384]{2,1,0:T(8,128)(2,1)} %get-tuple-element.99.rest_0_, bf16[16,96,384]{2,1,0:T(8,128)(2,1)} %get-tuple-element.98.rest_1_, ...), custom_call_target="tpu_custom_call", output_to_operand_aliasing={{1}: (13, {})} | custom-call | flops 38654705664 | bytes 18874368 | tf_op jit(solution)/shard_map/one_sided/pallas_call | solution.py:175
  640.2 6.3 place.6.rest_5_
  646.5 44.6 %full_terms.16 = (f32[16,96,768]{2,1,0:T(8,128)}, f32[8,96,1536]{2,1,0:T(8,128)}) custom-call(s32[32]{0:T(128)} %copy-done, s32[1]{0:T(128)} %bitcast.1.split_ref, bf16[8,16,96,384]{3,2,1,0:T(8,128)(2,1)} %bitcast.77, bf16[32,96,768]{2,1,0:T(8,128)(2,1)} %gather_fusion, ...), custom_call_target="tpu_custom_call", output_to_operand_aliasing={{0}: (9, {}), {1}: (10, {})} | custom-call | flops 33822867456 | bytes 18874368 | tf_op jit(solution)/shard_map/full_terms/pallas_call | solution.py:205
  691.1 44.5 %full_terms.17 = (f32[16,96,768]{2,1,0:T(8,128)}, f32[7,96,16,768]{3,2,1,0:T(8,128)}) custom-call(s32[32]{0:T(128)} %copy-done, s32[1]{0:T(128)} %bitcast.1.split_ref, bf16[8,16,96,384]{3,2,1,0:T(8,128)(2,1)} %bitcast.72, bf16[32,96,768]{2,1,0:T(8,128)(2,1)} %gather_fusion, ...), custom_call_target="tpu_custom_call", output_to_operand_aliasing={{0}: (9, {}), {1}: (10, {})} | custom-call | flops 33822867456 | bytes 18874368 | tf_op jit(solution)/shard_map/full_terms/pallas_call | solution.py:205
  735.5 16.1 %finish.8 = (f32[16,96,768]{2,1,0:T(8,128)}, bf16[16,96,384]{2,1,0:T(8,128)(2,1)}, bf16[16,96,384]{2,1,0:T(8,128)(2,1)}, f32[8,128]{1,0:T(8,128)}, f32[8,128]{1,0:T(8,128)}) custom-call(f32[1]{0:T(128)} %bitcast.13.beta_prev_ref, f32[16,96,768]{2,1,0:T(8,128)} %get-tuple-element.106.sigma_hbm, f32[16,96,768]{2,1,0:T(8,128)} %get-tuple-element.102.cur_hbm.prev_hbm, ...), custom_call_target="tpu_custom_call" | custom-call | flops 11796480 | bytes 25952256 | tf_op jit(solution)/shard_map/finish/pallas_call | solution.py:443
  752.4 3.3 all-to-all-start.2
  755.8 6.5 copy.76
  763.5 67.2 %all-to-all-done.2.rest_11_ = f32[8,96,1536]{2,1,0:T(8,128)} async-done(((f32[8,96,1536]{2,1,0:T(8,128)}), f32[8,96,1536]{2,1,0:T(8,128)}, u32[]{:S(2)}, u32[]{:S(2)}) %all-to-all-start.2) | async-done | bytes 4718624 | tf_op jit(solution)/shard_map/all_to_all | solution.py:506
  830.7 47.4 %one_sided.11 = (f32[16,96,768]{2,1,0:T(8,128)}, f32[8,96,1536]{2,1,0:T(8,128)}) custom-call(s32[32]{0:T(128)} %copy-done, s32[1]{0:T(128)} %bitcast.1.split_ref, bf16[16,96,384]{2,1,0:T(8,128)(2,1)} %get-tuple-element.109.rest_0_, bf16[16,96,384]{2,1,0:T(8,128)(2,1)} %get-tuple-element.108.rest_1_, ...), custom_call_target="tpu_custom_call", output_to_operand_aliasing={{1}: (13, {})} | custom-call | flops 38654705664 | bytes 18874368 | tf_op jit(solution)/shard_map/one_sided/pallas_call | solution.py:175
  878.2 6.3 place.7.rest_5_
  884.4 44.9 %full_terms.18 = (f32[16,96,768]{2,1,0:T(8,128)}, f32[8,96,1536]{2,1,0:T(8,128)}) custom-call(s32[32]{0:T(128)} %copy-done, s32[1]{0:T(128)} %bitcast.1.split_ref, bf16[8,16,96,384]{3,2,1,0:T(8,128)(2,1)} %bitcast.78, bf16[32,96,768]{2,1,0:T(8,128)(2,1)} %gather_fusion, ...), custom_call_target="tpu_custom_call", output_to_operand_aliasing={{0}: (9, {}), {1}: (10, {})} | custom-call | flops 33822867456 | bytes 18874368 | tf_op jit(solution)/shard_map/full_terms/pallas_call | solution.py:205
  929.3 44.6 %full_terms.19 = (f32[16,96,768]{2,1,0:T(8,128)}, f32[7,96,16,768]{3,2,1,0:T(8,128)}) custom-call(s32[32]{0:T(128)} %copy-done, s32[1]{0:T(128)} %bitcast.1.split_ref, bf16[8,16,96,384]{3,2,1,0:T(8,128)(2,1)} %bitcast.73, bf16[32,96,768]{2,1,0:T(8,128)(2,1)} %gather_fusion, ...), custom_call_target="tpu_custom_call", output_to_operand_aliasing={{0}: (9, {}), {1}: (10, {})} | custom-call | flops 33822867456 | bytes 18874368 | tf_op jit(solution)/shard_map/full_terms/pallas_call | solution.py:205
  973.9 15.9 %finish.9 = (f32[16,96,768]{2,1,0:T(8,128)}, bf16[16,96,384]{2,1,0:T(8,128)(2,1)}, bf16[16,96,384]{2,1,0:T(8,128)(2,1)}, f32[8,128]{1,0:T(8,128)}, f32[8,128]{1,0:T(8,128)}) custom-call(f32[1]{0:T(128)} %bitcast.19.beta_prev_ref, f32[16,96,768]{2,1,0:T(8,128)} %get-tuple-element.116.sigma_hbm, f32[16,96,768]{2,1,0:T(8,128)} %get-tuple-element.112.cur_hbm.prev_hbm, ...), custom_call_target="tpu_custom_call" | custom-call | flops 11796480 | bytes 25952256 | tf_op jit(solution)/shard_map/finish/pallas_call | solution.py:443
  990.4 3.4 all-to-all-start.3
  993.9 6.5 copy.77
  1001.7 67.5 %all-to-all-done.3.rest_11_ = f32[8,96,1536]{2,1,0:T(8,128)} async-done(((f32[8,96,1536]{2,1,0:T(8,128)}), f32[8,96,1536]{2,1,0:T(8,128)}, u32[]{:S(2)}, u32[]{:S(2)}) %all-to-all-start.3) | async-done | bytes 4718624 | tf_op jit(solution)/shard_map/all_to_all | solution.py:506
  1069.2 47.3 %one_sided.12 = (f32[16,96,768]{2,1,0:T(8,128)}, f32[8,96,1536]{2,1,0:T(8,128)}) custom-call(s32[32]{0:T(128)} %copy-done, s32[1]{0:T(128)} %bitcast.1.split_ref, bf16[16,96,384]{2,1,0:T(8,128)(2,1)} %get-tuple-element.119.rest_0_, bf16[16,96,384]{2,1,0:T(8,128)(2,1)} %get-tuple-element.118.rest_1_, ...), custom_call_target="tpu_custom_call", output_to_operand_aliasing={{1}: (13, {})} | custom-call | flops 38654705664 | bytes 18874368 | tf_op jit(solution)/shard_map/one_sided/pallas_call | solution.py:175
  1116.5 6.3 place.8.rest_5_
  1122.8 44.6 %full_terms.20 = (f32[16,96,768]{2,1,0:T(8,128)}, f32[8,96,1536]{2,1,0:T(8,128)}) custom-call(s32[32]{0:T(128)} %copy-done, s32[1]{0:T(128)} %bitcast.1.split_ref, bf16[8,16,96,384]{3,2,1,0:T(8,128)(2,1)} %bitcast.79, bf16[32,96,768]{2,1,0:T(8,128)(2,1)} %gather_fusion, ...), custom_call_target="tpu_custom_call", output_to_operand_aliasing={{0}: (9, {}), {1}: (10, {})} | custom-call | flops 33822867456 | bytes 18874368 | tf_op jit(solution)/shard_map/full_terms/pallas_call | solution.py:205
  1167.4 44.7 %full_terms.21 = (f32[16,96,768]{2,1,0:T(8,128)}, f32[7,96,16,768]{3,2,1,0:T(8,128)}) custom-call(s32[32]{0:T(128)} %copy-done, s32[1]{0:T(128)} %bitcast.1.split_ref, bf16[8,16,96,384]{3,2,1,0:T(8,128)(2,1)} %bitcast.74, bf16[32,96,768]{2,1,0:T(8,128)(2,1)} %gather_fusion, ...), custom_call_target="tpu_custom_call", output_to_operand_aliasing={{0}: (9, {}), {1}: (10, {})} | custom-call | flops 33822867456 | bytes 18874368 | tf_op jit(solution)/shard_map/full_terms/pallas_call | solution.py:205
  1212.1 16.0 %finish.10 = (f32[16,96,768]{2,1,0:T(8,128)}, bf16[16,96,384]{2,1,0:T(8,128)(2,1)}, bf16[16,96,384]{2,1,0:T(8,128)(2,1)}, f32[8,128]{1,0:T(8,128)}, f32[8,128]{1,0:T(8,128)}) custom-call(f32[1]{0:T(128)} %bitcast.25.beta_prev_ref, f32[16,96,768]{2,1,0:T(8,128)} %get-tuple-element.126.sigma_hbm, f32[16,96,768]{2,1,0:T(8,128)} %get-tuple-element.122.cur_hbm.prev_hbm, ...), custom_call_target="tpu_custom_call" | custom-call | flops 11796480 | bytes 25952256 | tf_op jit(solution)/shard_map/finish/pallas_call | solution.py:443
  1228.8 3.5 all-to-all-start.4
  1232.3 6.3 copy.78
  1238.6 68.7 %all-to-all-done.4.rest_11_ = f32[8,96,1536]{2,1,0:T(8,128)} async-done(((f32[8,96,1536]{2,1,0:T(8,128)}), f32[8,96,1536]{2,1,0:T(8,128)}, u32[]{:S(2)}, u32[]{:S(2)}) %all-to-all-start.4) | async-done | bytes 4718624 | tf_op jit(solution)/shard_map/all_to_all | solution.py:506
  1307.2 47.4 %one_sided.13 = (f32[16,96,768]{2,1,0:T(8,128)}, f32[8,96,1536]{2,1,0:T(8,128)}) custom-call(s32[32]{0:T(128)} %copy-done, s32[1]{0:T(128)} %bitcast.1.split_ref, bf16[16,96,384]{2,1,0:T(8,128)(2,1)} %get-tuple-element.129.rest_0_, bf16[16,96,384]{2,1,0:T(8,128)(2,1)} %get-tuple-element.128.rest_1_, ...), custom_call_target="tpu_custom_call", output_to_operand_aliasing={{1}: (13, {})} | custom-call | flops 38654705664 | bytes 18874368 | tf_op jit(solution)/shard_map/one_sided/pallas_call | solution.py:175
  1354.7 44.6 %full_terms.22 = (f32[16,96,768]{2,1,0:T(8,128)}, f32[8,96,1536]{2,1,0:T(8,128)}) custom-call(s32[32]{0:T(128)} %copy-done, s32[1]{0:T(128)} %bitcast.1.split_ref, bf16[8,16,96,384]{3,2,1,0:T(8,128)(2,1)} %bitcast.80, bf16[32,96,768]{2,1,0:T(8,128)(2,1)} %gather_fusion, ...), custom_call_target="tpu_custom_call", output_to_operand_aliasing={{0}: (9, {}), {1}: (10, {})} | custom-call | flops 33822867456 | bytes 18874368 | tf_op jit(solution)/shard_map/full_terms/pallas_call | solution.py:205
  1399.3 3.6 all-to-all-start.6
  1404.2 6.2 place.9.rest_5_
  1410.4 44.4 %full_terms.23 = (f32[16,96,768]{2,1,0:T(8,128)}, f32[7,96,16,768]{3,2,1,0:T(8,128)}) custom-call(s32[32]{0:T(128)} %copy-done, s32[1]{0:T(128)} %bitcast.1.split_ref, bf16[8,16,96,384]{3,2,1,0:T(8,128)(2,1)} %bitcast.71, bf16[32,96,768]{2,1,0:T(8,128)(2,1)} %gather_fusion, ...), custom_call_target="tpu_custom_call", output_to_operand_aliasing={{0}: (9, {}), {1}: (10, {})} | custom-call | flops 33822867456 | bytes 18874368 | tf_op jit(solution)/shard_map/full_terms/pallas_call | solution.py:205
  1454.8 16.7 %finish.11 = (f32[16,96,768]{2,1,0:T(8,128)}, bf16[16,96,384]{2,1,0:T(8,128)(2,1)}, bf16[16,96,384]{2,1,0:T(8,128)(2,1)}, f32[8,128]{1,0:T(8,128)}, f32[8,128]{1,0:T(8,128)}) custom-call(f32[1]{0:T(128)} %bitcast.31.beta_prev_ref, f32[16,96,768]{2,1,0:T(8,128)} %get-tuple-element.136.sigma_hbm, f32[16,96,768]{2,1,0:T(8,128)} %get-tuple-element.132.cur_hbm, ...), custom_call_target="tpu_custom_call" | custom-call | flops 11796480 | bytes 25952256 | tf_op jit(solution)/shard_map/finish/pallas_call | solution.py:443
  1471.5 6.1 copy.79
  1477.6 3.3 all-to-all-start.5
  1489.4 7.5 concatenate.7
  1498.1 6.2 place.10.refs_1_
  1504.3 31.3 %all-to-all-done.5.refs_0_ = f32[8,96,1536]{2,1,0:T(8,128)} async-done(((f32[8,96,1536]{2,1,0:T(8,128)}), f32[8,96,1536]{2,1,0:T(8,128)}, u32[]{:S(2)}, u32[]{:S(2)}) %all-to-all-start.5) | async-done | bytes 4718624 | tf_op jit(solution)/shard_map/all_to_all | solution.py:517
  1535.7 6.2 place.11
  (77 shorter events, 25.7 us)
Async XLA Ops:
  7.2 173.8 %all-gather.25.cloned.1.call-start = ((), (), s32[]{:S(2)}) async-start(), calls=%async_computation.8 | async-start | bytes 21233664 | tf_op jit(solution)/shard_map/all_gather | solution.py:473
  12.1 240.3 %all-gather.23.cloned.1.call-start = ((), (), s32[]{:S(2)}) async-start(), calls=%async_computation.7 | async-start | bytes 21233664 | tf_op jit(solution)/shard_map/all_gather | solution.py:473
  21.3 4.2 copy-start.2
  21.3 4.2 copy-start.1
  21.3 148.2 %all-to-all-start = ((bf16[4,768,768]{2,0,1:T(4,128)(2,1)}), bf16[4,768,768]{2,0,1:T(4,128)(2,1)}, u32[]{:S(2)}, u32[]{:S(2)}) async-start(bf16[4,768,768]{2,0,1:T(4,128)(2,1)} %copy.69), calls=%async_computation | async-start | bytes 9437184 | tf_op jit(solution)/shard_map/all_to_all | solution.py:470
  25.3 374.9 %all-gather.29.cloned.1.call-start = ((), (), s32[]{:S(2)}) async-start(), calls=%async_computation.10 | async-start | bytes 10616832 | tf_op jit(solution)/shard_map/all_gather | solution.py:513
  107.0 7.1 copy-start
  344.5 108.2 %all-gather.27.cloned.1.call-start = ((), (), s32[]{:S(2)}) async-start(), calls=%async_computation.9 | async-start | bytes 10616832 | tf_op jit(solution)/shard_map/all_gather | solution.py:513
  345.1 301.4 %all-gather.33.cloned.1.call-start = ((), (), s32[]{:S(2)}) async-start(), calls=%async_computation.12 | async-start | bytes 10616832 | tf_op jit(solution)/shard_map/all_gather | solution.py:513
  513.5 177.6 %all-gather.31.cloned.1.call-start = ((), (), s32[]{:S(2)}) async-start(), calls=%async_computation.11 | async-start | bytes 10616832 | tf_op jit(solution)/shard_map/all_gather | solution.py:513
  514.1 78.8 %all-to-all-start.1 = ((f32[8,96,1536]{2,1,0:T(8,128)}), f32[8,96,1536]{2,1,0:T(8,128)}, u32[]{:S(2)}, u32[]{:S(2)}) async-start(f32[8,96,1536]{2,1,0:T(8,128)} %get-tuple-element.100), calls=%async_computation.1 | async-start | bytes 9437184 | tf_op jit(solution)/shard_map/all_to_all | solution.py:506
  517.4 367.0 %all-gather.37.cloned.1.call-start = ((), (), s32[]{:S(2)}) async-start(), calls=%async_computation.14 | async-start | bytes 10616832 | tf_op jit(solution)/shard_map/all_gather | solution.py:513
  751.7 177.6 %all-gather.35.cloned.1.call-start = ((), (), s32[]{:S(2)}) async-start(), calls=%async_computation.13 | async-start | bytes 10616832 | tf_op jit(solution)/shard_map/all_gather | solution.py:513
  752.4 78.3 %all-to-all-start.2 = ((f32[8,96,1536]{2,1,0:T(8,128)}), f32[8,96,1536]{2,1,0:T(8,128)}, u32[]{:S(2)}, u32[]{:S(2)}) async-start(f32[8,96,1536]{2,1,0:T(8,128)} %get-tuple-element.110), calls=%async_computation.2 | async-start | bytes 9437184 | tf_op jit(solution)/shard_map/all_to_all | solution.py:506
  755.8 367.0 %all-gather.41.cloned.1.call-start = ((), (), s32[]{:S(2)}) async-start(), calls=%async_computation.16 | async-start | bytes 10616832 | tf_op jit(solution)/shard_map/all_gather | solution.py:513
  989.9 177.5 %all-gather.39.cloned.1.call-start = ((), (), s32[]{:S(2)}) async-start(), calls=%async_computation.15 | async-start | bytes 10616832 | tf_op jit(solution)/shard_map/all_gather | solution.py:513
  990.4 78.7 %all-to-all-start.3 = ((f32[8,96,1536]{2,1,0:T(8,128)}), f32[8,96,1536]{2,1,0:T(8,128)}, u32[]{:S(2)}, u32[]{:S(2)}) async-start(f32[8,96,1536]{2,1,0:T(8,128)} %get-tuple-element.120), calls=%async_computation.3 | async-start | bytes 9437184 | tf_op jit(solution)/shard_map/all_to_all | solution.py:506
  993.8 360.9 %all-gather.45.cloned.1.call-start = ((), (), s32[]{:S(2)}) async-start(), calls=%async_computation.18 | async-start | bytes 10616832 | tf_op jit(solution)/shard_map/all_gather | solution.py:513
  1228.2 182.2 %all-gather.43.cloned.1.call-start = ((), (), s32[]{:S(2)}) async-start(), calls=%async_computation.17 | async-start | bytes 10616832 | tf_op jit(solution)/shard_map/all_gather | solution.py:513
  1228.8 78.5 %all-to-all-start.4 = ((f32[8,96,1536]{2,1,0:T(8,128)}), f32[8,96,1536]{2,1,0:T(8,128)}, u32[]{:S(2)}, u32[]{:S(2)}) async-start(f32[8,96,1536]{2,1,0:T(8,128)} %get-tuple-element.130), calls=%async_computation.4 | async-start | bytes 9437184 | tf_op jit(solution)/shard_map/all_to_all | solution.py:506
  1399.3 78.3 %all-to-all-start.6 = ((f32[8,96,1536]{2,1,0:T(8,128)}), f32[8,96,1536]{2,1,0:T(8,128)}, u32[]{:S(2)}, u32[]{:S(2)}) async-start(f32[8,96,1536]{2,1,0:T(8,128)} %get-tuple-element.138), calls=%async_computation.6 | async-start | bytes 9437184 | tf_op jit(solution)/shard_map/all_to_all | solution.py:506
  1477.6 58.1 %all-to-all-start.5 = ((f32[8,96,1536]{2,1,0:T(8,128)}), f32[8,96,1536]{2,1,0:T(8,128)}, u32[]{:S(2)}, u32[]{:S(2)}) async-start(f32[8,96,1536]{2,1,0:T(8,128)} %bitcast.63), calls=%async_computation.5 | async-start | bytes 9437184 | tf_op jit(solution)/shard_map/all_to_all | solution.py:517
Sparse Core Ops, SparseCore 0:
  12.2 142.6 all-gather.24
  156.7 92.9 all-gather.22
  344.6 53.1 all-gather.28
  399.5 53.1 all-gather.26
  513.6 98.3 all-gather.32
  613.6 52.2 all-gather.30
  751.8 98.4 all-gather.36
  852.1 52.2 all-gather.34
  990.0 98.3 all-gather.40
  1090.0 52.2 all-gather.38
  1228.3 98.4 all-gather.44
  1328.5 52.2 all-gather.42

commit v2 on v1

--- a/solution.py
+++ b/solution.py
@@ -18,11 +18,22 @@
 FIN_BLOCKS = 4
 
 
-def one_sided_body(order_ref, split_ref, *rest, parts, resume):
+def stacked_left(refs, cuts):
+    rows, at = [], 0
+    for cut in cuts:
+        for t in range(GROUP):
+            pieces = [refs[at + t * cut + k][0] for k in range(cut)]
+            rows.append(pieces[0] if cut == 1 else jnp.concatenate(pieces, axis=1))
+        at += GROUP * cut
+    return jnp.concatenate(rows, axis=0)
+
+
+def one_sided_body(order_ref, split_ref, *rest, cuts, resume):
+    parts = len(cuts)
     u_refs = rest[:parts]
     pair_ref = rest[parts]
-    left_refs = rest[parts + 1:parts + 1 + GROUP * parts]
-    rest = rest[parts + 1 + GROUP * parts:]
+    left_refs = rest[parts + 1:parts + 1 + GROUP * sum(cuts)]
+    rest = rest[parts + 1 + GROUP * sum(cuts):]
     if resume:
         sigma_in, rest = rest[0], rest[1:]
     rest = rest[1:]
@@ -58,7 +69,7 @@
     for h in range(2):
         @pl.when(grp < split_ref[0])
         def _():
-            left = jnp.concatenate([left_refs[ci * GROUP + t][0] for ci in range(parts) for t in range(GROUP)], axis=0)
+            left = stacked_left(left_refs, cuts)
             zs = z_ref[h * half:(h + 1) * half].reshape(half * nb, parts * GROUP * nc)
             prod = jnp.dot(zs, left, preferred_element_type=F32).reshape(half, nb, na)
             sigma_ref[h * half:(h + 1) * half] += prod
@@ -73,9 +84,9 @@
             pltpu.make_async_copy(sigma_ref.at[pl.ds(h * half, half)], sigma_out.at[pl.ds(h * half, half)], out_sem.at[h]).wait()
 
 
-def full_body(order_ref, split_ref, u_hbm, right_ref, pair_ref, *rest, gathered, chunk):
-    left_refs = rest[:GROUP]
-    sigma_in, _, sigma_out, _, sigma_ref, u_ref, y_ref, z_ref, u_sem, in_sem, out_sem = rest[GROUP:]
+def full_body(order_ref, split_ref, u_hbm, right_ref, pair_ref, *rest, gathered, chunk, cut):
+    left_refs = rest[:GROUP * cut]
+    sigma_in, _, sigma_out, _, sigma_ref, u_ref, y_ref, z_ref, u_sem, in_sem, out_sem = rest[GROUP * cut:]
     grp = pl.program_id(0)
     num_grp = pl.num_programs(0)
     nq, nb, na = sigma_ref.shape
@@ -136,7 +147,7 @@
     for h in range(2):
         @pl.when(grp >= split_ref[0])
         def _():
-            left = jnp.concatenate([left_refs[t][0] for t in range(GROUP)], axis=0)
+            left = stacked_left(left_refs, (cut,))
             zs = z_ref[h * half:(h + 1) * half].reshape(half * nb, GROUP * nc)
             prod = jnp.dot(zs, left, preferred_element_type=F32).reshape(half, nb, na)
             sigma_ref[h * half:(h + 1) * half] += prod
@@ -159,21 +170,22 @@
     parts = len(u_parts)
     nq, nb, _ = u_parts[0][0].shape
     nc = CHUNK
-    na = left_parts[0].shape[2]
+    na = sum(piece.shape[2] for piece in left_parts[0])
+    cuts = tuple(len(part) for part in left_parts)
     terms = pair_blk.shape[0]
     nk = nq * ROW_TILE
 
     def clamp(g, s):
         return jnp.minimum(g, jnp.maximum(s[0] - 1, 0))
 
-    left_specs = [pl.BlockSpec((1, nc, na), functools.partial(lambda g, o, s, t: (o[clamp(g, s) * GROUP + t], 0, 0), t=t))
-                  for _ in range(parts) for t in range(GROUP)]
+    left_specs = [pl.BlockSpec((1,) + piece.shape[1:], functools.partial(lambda g, o, s, t: (o[clamp(g, s) * GROUP + t], 0, 0), t=t))
+                  for part in left_parts for t in range(GROUP) for piece in part]
     resume = sigma is not None
     n = terms // 2
-    first = 2 + parts + 1 + GROUP * parts
+    first = 2 + parts + 1 + GROUP * sum(cuts)
     aliases = {first: 0, first + 1: 1} if resume else {first: 1}
     return pl.pallas_call(
-        functools.partial(one_sided_body, parts=parts, resume=resume),
+        functools.partial(one_sided_body, cuts=cuts, resume=resume),
         grid_spec=pltpu.PrefetchScalarGridSpec(
             num_scalar_prefetch=2, grid=(terms // GROUP,),
             in_specs=[pl.BlockSpec((nq, nb, nc), functools.partial(lambda g, o, s, c: (0, 0, c), c=c), pipeline_mode=pl.Buffered(1)) for _, c in u_parts]
@@ -187,7 +199,7 @@
         compiler_params=pltpu.CompilerParams(dimension_semantics=('arbitrary',), vmem_limit_bytes=VMEM_LIMIT),
         cost_estimate=pl.CostEstimate(flops=n * 2 * nq * nb * parts * nc * (na + nk), bytes_accessed=n * na * nc * parts * 2, transcendentals=0),
         name='one_sided',
-    )(order, split, *[u for u, _ in u_parts], pair_blk, *[left_parts[c] for c in range(parts) for _ in range(GROUP)], *([sigma] if resume else []), carried)
+    )(order, split, *[u for u, _ in u_parts], pair_blk, *[piece for part in left_parts for _ in range(GROUP) for piece in part], *([sigma] if resume else []), carried)
 
 
 def full_call(order, split, u_part, chunk, right_slab, pair_blk, left_part, sigma, carried):
@@ -199,11 +211,12 @@
     def at_least(g, s):
         return jnp.minimum(jnp.maximum(g, s[0]), terms // GROUP - 1)
 
-    left_specs = [pl.BlockSpec((1, nc, na), functools.partial(lambda g, o, s, t: (o[at_least(g, s) * GROUP + t], 0, 0), t=t))
-                  for t in range(GROUP)]
+    left_specs = [pl.BlockSpec((1,) + piece.shape[1:], functools.partial(lambda g, o, s, t: (o[at_least(g, s) * GROUP + t], 0, 0), t=t))
+                  for t in range(GROUP) for piece in left_part]
+    cut = len(left_part)
     n = terms // 2
     return pl.pallas_call(
-        functools.partial(full_body, gathered=u_part.ndim == 4, chunk=chunk),
+        functools.partial(full_body, gathered=u_part.ndim == 4, chunk=chunk, cut=cut),
         grid_spec=pltpu.PrefetchScalarGridSpec(
             num_scalar_prefetch=2, grid=(terms // GROUP,),
             in_specs=[ANY,
@@ -214,11 +227,11 @@
                             pltpu.VMEM((nq, GROUP * nb, nc), BF16), pltpu.VMEM((nq, nb, GROUP * nc), BF16),
                             pltpu.SemaphoreType.DMA((nq,)), pltpu.SemaphoreType.DMA, pltpu.SemaphoreType.DMA((2,))]),
         out_shape=[jax.ShapeDtypeStruct((nq, nb, na), F32), jax.ShapeDtypeStruct(carried.shape, carried.dtype)],
-        input_output_aliases={2 + 3 + GROUP: 0, 2 + 4 + GROUP: 1},
+        input_output_aliases={2 + 3 + GROUP * cut: 0, 2 + 4 + GROUP * cut: 1},
         compiler_params=pltpu.CompilerParams(dimension_semantics=('arbitrary',), vmem_limit_bytes=VMEM_LIMIT),
         cost_estimate=pl.CostEstimate(flops=n * 2 * nq * nb * nc * (nd + na + nk), bytes_accessed=n * na * nc * 2 + nq * nd * nc * 2, transcendentals=0),
         name='full_terms',
-    )(order, split, u_part, right_slab, pair_blk, *[left_part] * GROUP, sigma, carried)
+    )(order, split, u_part, right_slab, pair_blk, *left_part * GROUP, sigma, carried)
 
 
 def place_body(*refs, num, nq, width):
@@ -462,15 +475,15 @@
         vec_size = wavefunction.size
         slab = bond // num
         me = lax.axis_index(AXIS_NAME)
-        nchunk = bond // CHUNK
+        nchunk = 2
 
         terms_loc = pair_loc.shape[0]
         small = jnp.concatenate([pair_loc.astype(F32).reshape(8, 128), jnp.pad(flag_loc.astype(F32), (0, 1024 - terms_loc)).reshape(8, 128)])
         small_all, norm_tile = exchange_call(small, wavefunction, num)
         right_slab = lax.all_to_all(right_loc, AXIS_NAME, split_axis=1, concat_axis=0, tiled=True)
-        left_parts = []
-        for i in range(nchunk):
-            left_parts.append(lax.all_gather(left_loc[:, i * CHUNK:(i + 1) * CHUNK], AXIS_NAME, axis=0, tiled=True))
+        top = lax.all_gather(left_loc[:, :CHUNK], AXIS_NAME, axis=0, tiled=True)
+        corner = lax.all_gather(left_loc[:, CHUNK:, CHUNK:], AXIS_NAME, axis=0, tiled=True)
+        left_parts = [(top,), (top[:, :, CHUNK:].transpose(0, 2, 1), corner)]
         pair_all = small_all[:, :8].reshape(num * terms_loc, nq, nq).astype(BF16)
         flags = small_all[:, 8, :terms_loc].reshape(-1).astype(jnp.int32)
         order = jnp.argsort(flags, stable=True).astype(jnp.int32)
@@ -490,11 +503,12 @@
         beta_prev = jnp.zeros((1,), F32)
         tiles = []
         leaving = arriving = None
+        sigma, krylov = one_sided_call(order, split, u_parts[:1], pair_blk, left_parts[:1], krylov)
         for step in range(LANCZOS_STEPS):
             if step == 0:
-                sigma = None
                 for i in range(nchunk):
-                    sigma, krylov = one_sided_call(order, split, u_parts[i:i + 1], pair_blk, left_parts[i:i + 1], krylov, sigma)
+                    if i:
+                        sigma, krylov = one_sided_call(order, split, u_parts[i:i + 1], pair_blk, left_parts[i:i + 1], krylov, sigma)
                     sigma, krylov = full_call(order, split, *u_wide[i], right_slab, pair_blk, left_parts[i], sigma, krylov)
             else:
                 if arriving is None:

time: 1560 us -> 1580 us (1.013)
  local copies, waits for them, and re-layouts: 112 us -> 135 us
  transfers between devices with their start and end apart: 19 -> 19, of which waited for: 6 -> 6; matrix products, arithmetic and copies ran while one was open for 8% -> 9% of each run, Pallas kernels for 47% -> 47%
where the time goes in v2:
time: 1580 us; the launch traced here: 1570 us
  Pallas kernels  1070 us (68%)
  waiting for transfers between devices  312 us (20%)
  local copies, waits for them, and re-layouts  135 us (9%)
  starting transfers between devices  25.9 us (2%)
  between operations  15.8 us (1%)
    pallas_call x12, Pallas kernels, full_call(): pl.pallas_call(functools.partial(full_body, gathered=u_part.ndim == 4, ch...  537 us
    all_to_all x6, waiting for transfers between devices, device_body(): lax.all_to_all(leaving, AXIS_NAME, split_axis=0, concat_axis=0, tiled=False)  302 us
    pallas_call x7, Pallas kernels, one_sided_call(): pl.pallas_call(functools.partial(one_sided_body, cuts=cuts, resume=resume...  295 us
    pallas_call x6, Pallas kernels, finish_call(): pl.pallas_call(functools.partial(finish_body, num=num, vec_size=vec_size)...  96.5 us
    pallas_call x1, Pallas kernels, exchange_call(): pl.pallas_call(functools.partial(exchange_body, num=num, vec_size=wavefun...  75 us
    reshape x6, local copies, waits for them, and re-layouts, device_body(): leaving = nxt.reshape(nq * slab, bond).T.reshape(num, slab, nq * slab)  38.4 us
    pallas_call x6, Pallas kernels, place_call(): pl.pallas_call(functools.partial(place_body, num=num, nq=nq, width=wide /...  37.5 us
  transfers between devices with their start and end apart: 19, of which 6 were waited for; matrix products, arithmetic and copies ran while one was open for 9% of the time, Pallas kernels for 47%

profile of v2, /device:TPU:0, one launch (start us, length us, event | category | flops | bytes accessed | tf_op | source)
XLA Modules:
  0.0 1572.8 jit_solution(6747191284128335394)
XLA Ops:
  7.2 3.2 slice.60
  13.0 8.1 copy.216
  21.1 4.5 all-to-all-start
  26.6 75.0 %exchange.1 = (f32[8,24,128]{2,1,0:T(8,128)}, f32[8,128]{1,0:T(8,128)}) custom-call(f32[16,128]{1,0:T(8,128)} %pad_maximum_fusion.x_ref, f32[768,16,768]{2,1,0:T(8,128)} %psi_ref.3), custom_call_target="tpu_custom_call" | custom-call | tf_op jit(solution)/shard_map/exchange/pallas_call | solution.py:322
  107.0 6.4 mul.24
  113.4 16.0 %copy.220 = bf16[32,256,256]{2,1,0:T(8,128)(2,1)} copy(bf16[32,256,256]{0,2,1:T(8,128)(2,1)} %bitcast.107) | data formatting | bytes 8388608 | tf_op jit(solution)/shard_map/mul | solution.py:495
  130.7 5.1 first.1.rest_6_
  135.8 27.6 %spread.1 = (bf16[16,768,768]{2,1,0:T(8,128)(2,1)}, f32[16,96,768]{2,1,0:T(8,128)}, bf16[16,96,768]{2,1,0:T(8,128)(2,1)}) custom-call(s32[1]{0:T(128)} %bitcast.2.me_ref, f32[8,128]{1,0:T(8,128)} %get-tuple-element.77.norm_ref, f32[768,16,768]{2,1,0:T(8,128)} %psi_ref.3), custom_call_target="tpu_custom_call" | custom-call | flops 9437184 | bytes 75497472 | tf_op jit(solution)/shard_map/spread/pallas_call | solution.py:346
  163.5 4.6 broadcast_multiply_fusion.rest_1_.pair_ref.rest_2_
  168.0 2.9 copy.217
  171.3 2.8 bitcast_select_fusion
  174.2 5.7 gather_fusion
  179.9 9.5 slice.82
  189.3 12.7 copy.228
  202.0 27.1 %one_sided.7 = (f32[16,96,768]{2,1,0:T(8,128)}, f32[7,96,16,768]{3,2,1,0:T(8,128)}) custom-call(s32[32]{0:T(128)} %copy-done, s32[1]{0:T(128)} %bitcast.1.split_ref, bf16[16,96,768]{2,1,0:T(8,128)(2,1)} %get-tuple-element.79.rest_0_, bf16[32,256,256]{2,1,0:T(8,128)(2,1)} %broadcast_multiply_fusion.rest_1_.pair_ref.rest_2_, ...), custom_call_target="tpu_custom_call", output_to_operand_aliasing={{1}: (8, {})} | custom-call | flops 19327352832 | bytes 9437184 | tf_op jit(solution)/shard_map/one_sided/pallas_call | solution.py:187
  229.1 44.3 %full_terms.12 = (f32[16,96,768]{2,1,0:T(8,128)}, f32[7,96,16,768]{3,2,1,0:T(8,128)}) custom-call(s32[32]{0:T(128)} %copy-done, s32[1]{0:T(128)} %bitcast.1.split_ref, bf16[16,768,768]{2,1,0:T(8,128)(2,1)} %get-tuple-element.78.u_hbm, bf16[32,96,768]{2,1,0:T(8,128)(2,1)} %gather_fusion, ...), custom_call_target="tpu_custom_call", output_to_operand_aliasing={{0}: (9, {}), {1}: (10, {})} | custom-call | flops 33822867456 | bytes 18874368 | tf_op jit(solution)/shard_map/full_terms/pallas_call | solution.py:218
  273.4 29.2 %one_sided.8 = (f32[16,96,768]{2,1,0:T(8,128)}, f32[7,96,16,768]{3,2,1,0:T(8,128)}) custom-call(s32[32]{0:T(128)} %copy-done, s32[1]{0:T(128)} %bitcast.1.split_ref, bf16[16,96,768]{2,1,0:T(8,128)(2,1)} %get-tuple-element.79.rest_0_, ...), custom_call_target="tpu_custom_call", output_to_operand_aliasing={{0}: (12, {}), {1}: (13, {})} | custom-call | flops 19327352832 | bytes 9437184 | tf_op jit(solution)/shard_map/one_sided/pallas_call | solution.py:187
  302.5 44.5 %full_terms.13 = (f32[16,96,768]{2,1,0:T(8,128)}, f32[7,96,16,768]{3,2,1,0:T(8,128)}) custom-call(s32[32]{0:T(128)} %copy-done, s32[1]{0:T(128)} %bitcast.1.split_ref, bf16[16,768,768]{2,1,0:T(8,128)(2,1)} %get-tuple-element.78.u_hbm, bf16[32,96,768]{2,1,0:T(8,128)(2,1)} %gather_fusion, ...), custom_call_target="tpu_custom_call", output_to_operand_aliasing={{0}: (13, {}), {1}: (14, {})} | custom-call | flops 33822867456 | bytes 18874368 | tf_op jit(solution)/shard_map/full_terms/pallas_call | solution.py:218
  349.8 15.6 finish.6
  366.0 6.4 copy.222
  373.6 47.6 %one_sided.9 = (f32[16,96,768]{2,1,0:T(8,128)}, f32[7,96,16,768]{3,2,1,0:T(8,128)}) custom-call(s32[32]{0:T(128)} %copy-done, s32[1]{0:T(128)} %bitcast.1.split_ref, bf16[16,96,384]{2,1,0:T(8,128)(2,1)} %get-tuple-element.90.rest_0_, bf16[16,96,384]{2,1,0:T(8,128)(2,1)} %get-tuple-element.89.rest_1_, ...), custom_call_target="tpu_custom_call", output_to_operand_aliasing={{1}: (17, {})} | custom-call | flops 38654705664 | bytes 18874368 | tf_op jit(solution)/shard_map/one_sided/pallas_call | solution.py:187
  421.2 45.5 %full_terms.14 = (f32[16,96,768]{2,1,0:T(8,128)}, f32[8,96,1536]{2,1,0:T(8,128)}) custom-call(s32[32]{0:T(128)} %copy-done, s32[1]{0:T(128)} %bitcast.1.split_ref, bf16[8,16,96,384]{3,2,1,0:T(8,128)(2,1)} %bitcast.130, bf16[32,96,768]{2,1,0:T(8,128)(2,1)} %gather_fusion, ...), custom_call_target="tpu_custom_call", output_to_operand_aliasing={{0}: (9, {}), {1}: (10, {})} | custom-call | flops 33822867456 | bytes 18874368 | tf_op jit(solution)/shard_map/full_terms/pallas_call | solution.py:218
  466.8 6.9 all-gather.27.cloned.1.call-done
  473.7 45.0 %full_terms.15 = (f32[16,96,768]{2,1,0:T(8,128)}, f32[7,96,16,768]{3,2,1,0:T(8,128)}) custom-call(s32[32]{0:T(128)} %copy-done, s32[1]{0:T(128)} %bitcast.1.split_ref, bf16[8,16,96,384]{3,2,1,0:T(8,128)(2,1)} %bitcast.124, bf16[32,96,768]{2,1,0:T(8,128)(2,1)} %gather_fusion, ...), custom_call_target="tpu_custom_call", output_to_operand_aliasing={{0}: (13, {}), {1}: (14, {})} | custom-call | flops 33822867456 | bytes 18874368 | tf_op jit(solution)/shard_map/full_terms/pallas_call | solution.py:218
  518.7 16.0 %finish.7 = (f32[16,96,768]{2,1,0:T(8,128)}, bf16[16,96,384]{2,1,0:T(8,128)(2,1)}, bf16[16,96,384]{2,1,0:T(8,128)(2,1)}, f32[8,128]{1,0:T(8,128)}, f32[8,128]{1,0:T(8,128)}) custom-call(f32[1]{0:T(128)} %bitcast.8.beta_prev_ref, f32[16,96,768]{2,1,0:T(8,128)} %get-tuple-element.96.sigma_hbm, f32[16,96,768]{2,1,0:T(8,128)} %get-tuple-element.93.cur_hbm.prev_hbm, ...), custom_call_target="tpu_custom_call" | custom-call | flops 11796480 | bytes 25952256 | tf_op jit(solution)/shard_map/finish/pallas_call | solution.py:456
  535.4 3.4 all-to-all-start.1
  538.8 6.6 copy.223
  546.6 67.7 %all-to-all-done.1.rest_15_ = f32[8,96,1536]{2,1,0:T(8,128)} async-done(((f32[8,96,1536]{2,1,0:T(8,128)}), f32[8,96,1536]{2,1,0:T(8,128)}, u32[]{:S(2)}, u32[]{:S(2)}) %all-to-all-start.1) | async-done | bytes 4718624 | tf_op jit(solution)/shard_map/all_to_all | solution.py:520
  614.3 47.7 %one_sided.10 = (f32[16,96,768]{2,1,0:T(8,128)}, f32[8,96,1536]{2,1,0:T(8,128)}) custom-call(s32[32]{0:T(128)} %copy-done, s32[1]{0:T(128)} %bitcast.1.split_ref, bf16[16,96,384]{2,1,0:T(8,128)(2,1)} %get-tuple-element.99.rest_0_, bf16[16,96,384]{2,1,0:T(8,128)(2,1)} %get-tuple-element.98.rest_1_, ...), custom_call_target="tpu_custom_call", output_to_operand_aliasing={{1}: (17, {})} | custom-call | flops 38654705664 | bytes 18874368 | tf_op jit(solution)/shard_map/one_sided/pallas_call | solution.py:187
  662.0 6.2 place.6.rest_9_
  668.2 44.7 %full_terms.16 = (f32[16,96,768]{2,1,0:T(8,128)}, f32[8,96,1536]{2,1,0:T(8,128)}) custom-call(s32[32]{0:T(128)} %copy-done, s32[1]{0:T(128)} %bitcast.1.split_ref, bf16[8,16,96,384]{3,2,1,0:T(8,128)(2,1)} %bitcast.126, bf16[32,96,768]{2,1,0:T(8,128)(2,1)} %gather_fusion, ...), custom_call_target="tpu_custom_call", output_to_operand_aliasing={{0}: (9, {}), {1}: (10, {})} | custom-call | flops 33822867456 | bytes 18874368 | tf_op jit(solution)/shard_map/full_terms/pallas_call | solution.py:218
  712.9 44.8 %full_terms.17 = (f32[16,96,768]{2,1,0:T(8,128)}, f32[7,96,16,768]{3,2,1,0:T(8,128)}) custom-call(s32[32]{0:T(128)} %copy-done, s32[1]{0:T(128)} %bitcast.1.split_ref, bf16[8,16,96,384]{3,2,1,0:T(8,128)(2,1)} %bitcast.121, bf16[32,96,768]{2,1,0:T(8,128)(2,1)} %gather_fusion, ...), custom_call_target="tpu_custom_call", output_to_operand_aliasing={{0}: (13, {}), {1}: (14, {})} | custom-call | flops 33822867456 | bytes 18874368 | tf_op jit(solution)/shard_map/full_terms/pallas_call | solution.py:218
  757.8 16.0 %finish.8 = (f32[16,96,768]{2,1,0:T(8,128)}, bf16[16,96,384]{2,1,0:T(8,128)(2,1)}, bf16[16,96,384]{2,1,0:T(8,128)(2,1)}, f32[8,128]{1,0:T(8,128)}, f32[8,128]{1,0:T(8,128)}) custom-call(f32[1]{0:T(128)} %bitcast.14.beta_prev_ref, f32[16,96,768]{2,1,0:T(8,128)} %get-tuple-element.106.sigma_hbm, f32[16,96,768]{2,1,0:T(8,128)} %get-tuple-element.102.cur_hbm.prev_hbm, ...), custom_call_target="tpu_custom_call" | custom-call | flops 11796480 | bytes 25952256 | tf_op jit(solution)/shard_map/finish/pallas_call | solution.py:456
  774.5 3.3 all-to-all-start.2
  777.9 6.7 copy.224
  785.8 67.1 %all-to-all-done.2.rest_15_ = f32[8,96,1536]{2,1,0:T(8,128)} async-done(((f32[8,96,1536]{2,1,0:T(8,128)}), f32[8,96,1536]{2,1,0:T(8,128)}, u32[]{:S(2)}, u32[]{:S(2)}) %all-to-all-start.2) | async-done | bytes 4718624 | tf_op jit(solution)/shard_map/all_to_all | solution.py:520
  852.8 47.7 %one_sided.11 = (f32[16,96,768]{2,1,0:T(8,128)}, f32[8,96,1536]{2,1,0:T(8,128)}) custom-call(s32[32]{0:T(128)} %copy-done, s32[1]{0:T(128)} %bitcast.1.split_ref, bf16[16,96,384]{2,1,0:T(8,128)(2,1)} %get-tuple-element.109.rest_0_, bf16[16,96,384]{2,1,0:T(8,128)(2,1)} %get-tuple-element.108.rest_1_, ...), custom_call_target="tpu_custom_call", output_to_operand_aliasing={{1}: (17, {})} | custom-call | flops 38654705664 | bytes 18874368 | tf_op jit(solution)/shard_map/one_sided/pallas_call | solution.py:187
  900.5 6.3 place.7.rest_9_
  906.8 44.5 %full_terms.18 = (f32[16,96,768]{2,1,0:T(8,128)}, f32[8,96,1536]{2,1,0:T(8,128)}) custom-call(s32[32]{0:T(128)} %copy-done, s32[1]{0:T(128)} %bitcast.1.split_ref, bf16[8,16,96,384]{3,2,1,0:T(8,128)(2,1)} %bitcast.127, bf16[32,96,768]{2,1,0:T(8,128)(2,1)} %gather_fusion, ...), custom_call_target="tpu_custom_call", output_to_operand_aliasing={{0}: (9, {}), {1}: (10, {})} | custom-call | flops 33822867456 | bytes 18874368 | tf_op jit(solution)/shard_map/full_terms/pallas_call | solution.py:218
  951.3 44.8 %full_terms.19 = (f32[16,96,768]{2,1,0:T(8,128)}, f32[7,96,16,768]{3,2,1,0:T(8,128)}) custom-call(s32[32]{0:T(128)} %copy-done, s32[1]{0:T(128)} %bitcast.1.split_ref, bf16[8,16,96,384]{3,2,1,0:T(8,128)(2,1)} %bitcast.122, bf16[32,96,768]{2,1,0:T(8,128)(2,1)} %gather_fusion, ...), custom_call_target="tpu_custom_call", output_to_operand_aliasing={{0}: (13, {}), {1}: (14, {})} | custom-call | flops 33822867456 | bytes 18874368 | tf_op jit(solution)/shard_map/full_terms/pallas_call | solution.py:218
  996.1 16.0 %finish.9 = (f32[16,96,768]{2,1,0:T(8,128)}, bf16[16,96,384]{2,1,0:T(8,128)(2,1)}, bf16[16,96,384]{2,1,0:T(8,128)(2,1)}, f32[8,128]{1,0:T(8,128)}, f32[8,128]{1,0:T(8,128)}) custom-call(f32[1]{0:T(128)} %bitcast.20.beta_prev_ref, f32[16,96,768]{2,1,0:T(8,128)} %get-tuple-element.116.sigma_hbm, f32[16,96,768]{2,1,0:T(8,128)} %get-tuple-element.112.cur_hbm.prev_hbm, ...), custom_call_target="tpu_custom_call" | custom-call | flops 11796480 | bytes 25952256 | tf_op jit(solution)/shard_map/finish/pallas_call | solution.py:456
  1012.7 3.4 all-to-all-start.3
  1016.1 6.5 copy.225
  1023.9 67.5 %all-to-all-done.3.rest_15_ = f32[8,96,1536]{2,1,0:T(8,128)} async-done(((f32[8,96,1536]{2,1,0:T(8,128)}), f32[8,96,1536]{2,1,0:T(8,128)}, u32[]{:S(2)}, u32[]{:S(2)}) %all-to-all-start.3) | async-done | bytes 4718624 | tf_op jit(solution)/shard_map/all_to_all | solution.py:520
  1091.4 47.7 %one_sided.12 = (f32[16,96,768]{2,1,0:T(8,128)}, f32[8,96,1536]{2,1,0:T(8,128)}) custom-call(s32[32]{0:T(128)} %copy-done, s32[1]{0:T(128)} %bitcast.1.split_ref, bf16[16,96,384]{2,1,0:T(8,128)(2,1)} %get-tuple-element.119.rest_0_, bf16[16,96,384]{2,1,0:T(8,128)(2,1)} %get-tuple-element.118.rest_1_, ...), custom_call_target="tpu_custom_call", output_to_operand_aliasing={{1}: (17, {})} | custom-call | flops 38654705664 | bytes 18874368 | tf_op jit(solution)/shard_map/one_sided/pallas_call | solution.py:187
  1139.1 6.3 place.8.rest_9_
  1145.3 44.9 %full_terms.20 = (f32[16,96,768]{2,1,0:T(8,128)}, f32[8,96,1536]{2,1,0:T(8,128)}) custom-call(s32[32]{0:T(128)} %copy-done, s32[1]{0:T(128)} %bitcast.1.split_ref, bf16[8,16,96,384]{3,2,1,0:T(8,128)(2,1)} %bitcast.128, bf16[32,96,768]{2,1,0:T(8,128)(2,1)} %gather_fusion, ...), custom_call_target="tpu_custom_call", output_to_operand_aliasing={{0}: (9, {}), {1}: (10, {})} | custom-call | flops 33822867456 | bytes 18874368 | tf_op jit(solution)/shard_map/full_terms/pallas_call | solution.py:218
  1190.3 44.8 %full_terms.21 = (f32[16,96,768]{2,1,0:T(8,128)}, f32[7,96,16,768]{3,2,1,0:T(8,128)}) custom-call(s32[32]{0:T(128)} %copy-done, s32[1]{0:T(128)} %bitcast.1.split_ref, bf16[8,16,96,384]{3,2,1,0:T(8,128)(2,1)} %bitcast.123, bf16[32,96,768]{2,1,0:T(8,128)(2,1)} %gather_fusion, ...), custom_call_target="tpu_custom_call", output_to_operand_aliasing={{0}: (13, {}), {1}: (14, {})} | custom-call | flops 33822867456 | bytes 18874368 | tf_op jit(solution)/shard_map/full_terms/pallas_call | solution.py:218
  1235.1 16.1 %finish.10 = (f32[16,96,768]{2,1,0:T(8,128)}, bf16[16,96,384]{2,1,0:T(8,128)(2,1)}, bf16[16,96,384]{2,1,0:T(8,128)(2,1)}, f32[8,128]{1,0:T(8,128)}, f32[8,128]{1,0:T(8,128)}) custom-call(f32[1]{0:T(128)} %bitcast.26.beta_prev_ref, f32[16,96,768]{2,1,0:T(8,128)} %get-tuple-element.126.sigma_hbm, f32[16,96,768]{2,1,0:T(8,128)} %get-tuple-element.122.cur_hbm.prev_hbm, ...), custom_call_target="tpu_custom_call" | custom-call | flops 11796480 | bytes 25952256 | tf_op jit(solution)/shard_map/finish/pallas_call | solution.py:456
  1251.7 3.6 all-to-all-start.4
  1255.3 6.2 copy.226
  1261.5 68.7 %all-to-all-done.4.rest_15_ = f32[8,96,1536]{2,1,0:T(8,128)} async-done(((f32[8,96,1536]{2,1,0:T(8,128)}), f32[8,96,1536]{2,1,0:T(8,128)}, u32[]{:S(2)}, u32[]{:S(2)}) %all-to-all-start.4) | async-done | bytes 4718624 | tf_op jit(solution)/shard_map/all_to_all | solution.py:520
  1330.2 47.7 %one_sided.13 = (f32[16,96,768]{2,1,0:T(8,128)}, f32[8,96,1536]{2,1,0:T(8,128)}) custom-call(s32[32]{0:T(128)} %copy-done, s32[1]{0:T(128)} %bitcast.1.split_ref, bf16[16,96,384]{2,1,0:T(8,128)(2,1)} %get-tuple-element.129.rest_0_, bf16[16,96,384]{2,1,0:T(8,128)(2,1)} %get-tuple-element.128.rest_1_, ...), custom_call_target="tpu_custom_call", output_to_operand_aliasing={{1}: (17, {})} | custom-call | flops 38654705664 | bytes 18874368 | tf_op jit(solution)/shard_map/one_sided/pallas_call | solution.py:187
  1377.9 44.7 %full_terms.22 = (f32[16,96,768]{2,1,0:T(8,128)}, f32[8,96,1536]{2,1,0:T(8,128)}) custom-call(s32[32]{0:T(128)} %copy-done, s32[1]{0:T(128)} %bitcast.1.split_ref, bf16[8,16,96,384]{3,2,1,0:T(8,128)(2,1)} %bitcast.129, bf16[32,96,768]{2,1,0:T(8,128)(2,1)} %gather_fusion, ...), custom_call_target="tpu_custom_call", output_to_operand_aliasing={{0}: (9, {}), {1}: (10, {})} | custom-call | flops 33822867456 | bytes 18874368 | tf_op jit(solution)/shard_map/full_terms/pallas_call | solution.py:218
  1422.6 3.7 all-to-all-start.6
  1427.5 6.2 place.9.rest_9_
  1433.8 44.6 %full_terms.23 = (f32[16,96,768]{2,1,0:T(8,128)}, f32[7,96,16,768]{3,2,1,0:T(8,128)}) custom-call(s32[32]{0:T(128)} %copy-done, s32[1]{0:T(128)} %bitcast.1.split_ref, bf16[8,16,96,384]{3,2,1,0:T(8,128)(2,1)} %bitcast.120, bf16[32,96,768]{2,1,0:T(8,128)(2,1)} %gather_fusion, ...), custom_call_target="tpu_custom_call", output_to_operand_aliasing={{0}: (13, {}), {1}: (14, {})} | custom-call | flops 33822867456 | bytes 18874368 | tf_op jit(solution)/shard_map/full_terms/pallas_call | solution.py:218
  1478.3 16.7 %finish.11 = (f32[16,96,768]{2,1,0:T(8,128)}, bf16[16,96,384]{2,1,0:T(8,128)(2,1)}, bf16[16,96,384]{2,1,0:T(8,128)(2,1)}, f32[8,128]{1,0:T(8,128)}, f32[8,128]{1,0:T(8,128)}) custom-call(f32[1]{0:T(128)} %bitcast.32.beta_prev_ref, f32[16,96,768]{2,1,0:T(8,128)} %get-tuple-element.136.sigma_hbm, f32[16,96,768]{2,1,0:T(8,128)} %get-tuple-element.132.cur_hbm, ...), custom_call_target="tpu_custom_call" | custom-call | flops 11796480 | bytes 25952256 | tf_op jit(solution)/shard_map/finish/pallas_call | solution.py:456
  1495.1 6.1 copy.227
  1501.2 3.3 all-to-all-start.5
  1513.2 7.7 concatenate.7
  1522.1 6.2 place.10.refs_1_
  1528.3 30.9 %all-to-all-done.5.refs_0_ = f32[8,96,1536]{2,1,0:T(8,128)} async-done(((f32[8,96,1536]{2,1,0:T(8,128)}), f32[8,96,1536]{2,1,0:T(8,128)}, u32[]{:S(2)}, u32[]{:S(2)}) %all-to-all-start.5) | async-done | bytes 4718624 | tf_op jit(solution)/shard_map/all_to_all | solution.py:531
  1559.2 6.2 place.11
  (80 shorter events, 31.9 us)
Async XLA Ops:
  7.2 172.7 %all-gather.23.cloned.1.call-start = ((), (), s32[]{:S(2)}) async-start(), calls=%async_computation.7 | async-start | bytes 21233664 | tf_op jit(solution)/shard_map/all_gather | solution.py:484
  10.5 262.9 %all-gather.25.cloned.1.call-start = ((), (), s32[]{:S(2)}) async-start(), calls=%async_computation.8 | async-start | bytes 10616832 | tf_op jit(solution)/shard_map/all_gather | solution.py:485
  21.1 4.7 copy-start.2
  21.1 4.8 copy-start.1
  21.1 146.9 %all-to-all-start = ((bf16[4,768,768]{2,0,1:T(4,128)(2,1)}), bf16[4,768,768]{2,0,1:T(4,128)(2,1)}, u32[]{:S(2)}, u32[]{:S(2)}) async-start(bf16[4,768,768]{2,0,1:T(4,128)(2,1)} %copy.216), calls=%async_computation | async-start | bytes 9437184 | tf_op jit(solution)/shard_map/all_to_all | solution.py:483
  25.6 395.7 %all-gather.29.cloned.1.call-start = ((), (), s32[]{:S(2)}) async-start(), calls=%async_computation.10 | async-start | bytes 10616832 | tf_op jit(solution)/shard_map/all_gather | solution.py:527
  106.3 7.1 copy-start
  365.4 108.3 %all-gather.27.cloned.1.call-start = ((), (), s32[]{:S(2)}) async-start(), calls=%async_computation.9 | async-start | bytes 10616832 | tf_op jit(solution)/shard_map/all_gather | solution.py:527
  366.0 302.2 %all-gather.33.cloned.1.call-start = ((), (), s32[]{:S(2)}) async-start(), calls=%async_computation.12 | async-start | bytes 10616832 | tf_op jit(solution)/shard_map/all_gather | solution.py:527
  534.8 178.1 %all-gather.31.cloned.1.call-start = ((), (), s32[]{:S(2)}) async-start(), calls=%async_computation.11 | async-start | bytes 10616832 | tf_op jit(solution)/shard_map/all_gather | solution.py:527
  535.4 78.9 %all-to-all-start.1 = ((f32[8,96,1536]{2,1,0:T(8,128)}), f32[8,96,1536]{2,1,0:T(8,128)}, u32[]{:S(2)}, u32[]{:S(2)}) async-start(f32[8,96,1536]{2,1,0:T(8,128)} %get-tuple-element.100), calls=%async_computation.1 | async-start | bytes 9437184 | tf_op jit(solution)/shard_map/all_to_all | solution.py:520
  538.8 368.0 %all-gather.37.cloned.1.call-start = ((), (), s32[]{:S(2)}) async-start(), calls=%async_computation.14 | async-start | bytes 10616832 | tf_op jit(solution)/shard_map/all_gather | solution.py:527
  773.8 177.5 %all-gather.35.cloned.1.call-start = ((), (), s32[]{:S(2)}) async-start(), calls=%async_computation.13 | async-start | bytes 10616832 | tf_op jit(solution)/shard_map/all_gather | solution.py:527
  774.5 78.3 %all-to-all-start.2 = ((f32[8,96,1536]{2,1,0:T(8,128)}), f32[8,96,1536]{2,1,0:T(8,128)}, u32[]{:S(2)}, u32[]{:S(2)}) async-start(f32[8,96,1536]{2,1,0:T(8,128)} %get-tuple-element.110), calls=%async_computation.2 | async-start | bytes 9437184 | tf_op jit(solution)/shard_map/all_to_all | solution.py:520
  777.9 367.4 %all-gather.41.cloned.1.call-start = ((), (), s32[]{:S(2)}) async-start(), calls=%async_computation.16 | async-start | bytes 10616832 | tf_op jit(solution)/shard_map/all_gather | solution.py:527
  1012.1 178.2 %all-gather.39.cloned.1.call-start = ((), (), s32[]{:S(2)}) async-start(), calls=%async_computation.15 | async-start | bytes 10616832 | tf_op jit(solution)/shard_map/all_gather | solution.py:527
  1012.7 78.6 %all-to-all-start.3 = ((f32[8,96,1536]{2,1,0:T(8,128)}), f32[8,96,1536]{2,1,0:T(8,128)}, u32[]{:S(2)}, u32[]{:S(2)}) async-start(f32[8,96,1536]{2,1,0:T(8,128)} %get-tuple-element.120), calls=%async_computation.3 | async-start | bytes 9437184 | tf_op jit(solution)/shard_map/all_to_all | solution.py:520
  1016.1 361.8 %all-gather.45.cloned.1.call-start = ((), (), s32[]{:S(2)}) async-start(), calls=%async_computation.18 | async-start | bytes 10616832 | tf_op jit(solution)/shard_map/all_gather | solution.py:527
  1251.2 182.6 %all-gather.43.cloned.1.call-start = ((), (), s32[]{:S(2)}) async-start(), calls=%async_computation.17 | async-start | bytes 10616832 | tf_op jit(solution)/shard_map/all_gather | solution.py:527
  1251.7 78.5 %all-to-all-start.4 = ((f32[8,96,1536]{2,1,0:T(8,128)}), f32[8,96,1536]{2,1,0:T(8,128)}, u32[]{:S(2)}, u32[]{:S(2)}) async-start(f32[8,96,1536]{2,1,0:T(8,128)} %get-tuple-element.130), calls=%async_computation.4 | async-start | bytes 9437184 | tf_op jit(solution)/shard_map/all_to_all | solution.py:520
  1422.6 78.6 %all-to-all-start.6 = ((f32[8,96,1536]{2,1,0:T(8,128)}), f32[8,96,1536]{2,1,0:T(8,128)}, u32[]{:S(2)}, u32[]{:S(2)}) async-start(f32[8,96,1536]{2,1,0:T(8,128)} %get-tuple-element.138), calls=%async_computation.6 | async-start | bytes 9437184 | tf_op jit(solution)/shard_map/all_to_all | solution.py:520
  1501.2 58.1 %all-to-all-start.5 = ((f32[8,96,1536]{2,1,0:T(8,128)}), f32[8,96,1536]{2,1,0:T(8,128)}, u32[]{:S(2)}, u32[]{:S(2)}) async-start(f32[8,96,1536]{2,1,0:T(8,128)} %bitcast.112), calls=%async_computation.5 | async-start | bytes 9437184 | tf_op jit(solution)/shard_map/all_to_all | solution.py:531
Sparse Core Ops, SparseCore 0:
  10.6 142.6 all-gather.22
  155.1 53.1 all-gather.24
  365.5 53.2 all-gather.28
  420.5 53.1 all-gather.26
  534.9 98.3 all-gather.32
  635.0 52.2 all-gather.30
  773.9 98.4 all-gather.36
  874.2 52.2 all-gather.34
  1012.3 98.3 all-gather.40
  1112.3 52.2 all-gather.38
  1251.3 98.4 all-gather.44
  1351.5 52.2 all-gather.42
